TPU v7x, 32 devices: a whole 2x2x4 slice. The times are simulated.
32 devices in a mesh: gx: 4 (over y, x), gy: 4 (over z), gz: 2 (over core).
Axes of the slice: x: 2, y: 2, z: 4, core: 2. Of those that a mesh axis runs over, the one named last changes fastest.
Arguments:
- residual: float32 [3, 32, 256, 512], P(None, 'gz', 'gx', 'gy'), may hold values from -32 to 32
- edge_diag: float32 [3, 32, 256, 512], P(None, 'gz', 'gx', 'gy'), may hold values from 6.5 to 9
- node_shift: float32 [32, 256, 512], P('gz', 'gx', 'gy'), may hold values from 0.05 to 3
- coarse_shift: float32 [16, 128, 256], P('gz', 'gx', 'gy'), may hold values from 0.05 to 3
Outputs:
- correction: float32 [3, 32, 256, 512], P(None, 'gz', 'gx', 'gy')
All inputs are finite; a program needn't handle non-finite values.
Results may differ from a plain program's by a relative error of at most 0.000021.
Values sent between devices are 32-bit elements; how exact they have to be, the bound alone decides.
A program may use at most 128 MiB of HBM per device.

v0:
```python
import functools
import itertools
import math

import jax
import jax.numpy as jnp
from jax import lax
from jax.experimental import pallas as pl
from jax.experimental.pallas import tpu as pltpu
from jax.sharding import PartitionSpec as P

MESH = pl.DeviceIdType.MESH
AXES = ("gz", "gx", "gy")
FGI, V1I, V2I, F0I = 3, 4, 5, 6
PAD = 8
PHASES = ((1, 2), (0,))


def kernel(
    sizes,
    res, dia, shf, csh, OB,
    R, D, NI, CS, S, FG, CI, CR, A1, T, V1, V2, F, FN,
    SX, RX, SY, RY, PA, PB,
    in_sem, send_sem, recv_sem, psend, precv,
):
    n0, n1, n2 = NI.shape
    m0, m1, m2 = CS.shape
    groups = n1 // 8
    me = [lax.axis_index(a) for a in AXES]
    rows = pl.ds(PAD, n1)

    def offsets(axes):
        every = itertools.product(*[range(sizes[a]) for a in axes])
        return [offs for offs in every if any(offs)]

    def partner(axes, offs, sign):
        return {
            AXES[a]: lax.rem(me[a] + (o if sign > 0 else sizes[a] - o), sizes[a]) for a, o in zip(axes, offs)
        }

    loads = []
    for k in (1, 2, 0):
        for src, dst in ((res, R), (dia, D)):
            loads.append(pltpu.make_async_copy(src.at[k], dst.at[k], in_sem.at[len(loads)]))
    loads.append(pltpu.make_async_copy(shf, NI, in_sem.at[6]))
    loads.append(pltpu.make_async_copy(csh, CS, in_sem.at[7]))
    for c in loads:
        c.start()

    zplane = jnp.zeros((n1, n2), jnp.float32)
    for k in range(3):
        S[k, 0, rows] = zplane
        S[k, n0 + 1, rows] = zplane
        F[k, n0] = zplane
    FG[0, rows] = zplane
    FG[n0 + 1, rows] = zplane
    for V in (V1, V2):
        V[0, rows] = zplane
        V[m0 + 1, rows] = zplane
    RX[...] = jnp.zeros(RX.shape, jnp.float32)
    RY[...] = jnp.zeros(RY.shape, jnp.float32)
    barrier = pltpu.get_barrier_semaphore()
    total = 0
    for axes in PHASES:
        for offs in offsets(axes):
            pl.semaphore_signal(barrier, inc=1, device_id=partner(axes, offs, 1), device_id_type=MESH)
            total += 1

    lane = lax.broadcasted_iota(jnp.int32, (8, n2), 1)
    lane_full = lax.broadcasted_iota(jnp.int32, (n1, n2), 1)
    row_full = lax.broadcasted_iota(jnp.int32, (n1, n2), 0)
    row8 = lax.broadcasted_iota(jnp.int32, (8, n2), 0)
    keys = {p: ((lane + p // 2) // p) % (n2 // p) for p in (2, 4)}
    is_low = {p: (lane % p) >= p // 2 for p in (2, 4)}

    def place(i, g, p):
        k = i * groups + g
        per = n2 // p
        return k // per, k % per

    def pack(f, plane, count, p):
        accs = [jnp.zeros((8, n2), jnp.float32) for _ in range(place(count - 1, groups - 1, p)[0] + 1)]
        for i in range(count):
            x = plane(i)
            for g in range(groups):
                v, kk = place(i, g, p)
                part = x[8 * g : 8 * g + 8]
                if kk:
                    part = pltpu.roll(part, p * kk, 1)
                accs[v] = jnp.where(keys[p] == kk, part, accs[v])
        for v, acc in enumerate(accs):
            SY[f, v] = acc

    def arrived(f, p):
        return [jnp.where(is_low[p], RY[f, 0, v], RY[f, 1, v]) for v in range(RY.shape[2])]

    def halo(ws, i, p):
        parts = []
        for g in range(groups):
            v, kk = place(i, g, p)
            parts.append(pltpu.roll(ws[v], n2 - p * kk, 1) if kk else ws[v])
        return jnp.concatenate(parts, axis=0)

    def from_low(x, h, sh=1):
        return pltpu.roll(jnp.where(lane_full >= n2 - sh, h, x), sh, 1)

    def from_high(x, h, sh=1):
        return pltpu.roll(jnp.where(lane_full < sh, h, x), n2 - sh, 1)

    def inplane(ref, x, h, sh):
        near = ref[pl.ds(PAD - sh, n1)] + ref[pl.ds(PAD + sh, n1)]
        return near + from_low(x, h, sh) + from_high(x, h, sh)

    def local_near(ref, i, n, sh):
        x = ref[1 + i, rows]
        near = jnp.where(row_full >= sh, ref[1 + i, pl.ds(PAD - sh, n1)], 0.0)
        near = near + jnp.where(row_full < n1 - sh, ref[1 + i, pl.ds(PAD + sh, n1)], 0.0)
        near = near + jnp.where(lane_full >= sh, pltpu.roll(x, sh, 1), 0.0)
        near = near + jnp.where(lane_full < n2 - sh, pltpu.roll(x, n2 - sh, 1), 0.0)
        if i > 0:
            near = near + ref[i, rows]
        if i < n - 1:
            near = near + ref[i + 2, rows]
        return near

    def edges(f, p):
        sh = p // 2
        return [
            jnp.where(is_low[p], pltpu.roll(RY[f, 1, v], n2 - sh, 1), pltpu.roll(RY[f, 0, v], sh, 1))
            for v in range(RY.shape[2])
        ]

    def outer_near(near, ref, f, ws, i, n, p):
        sh = p // 2
        if i == 0:
            near = near + ref[0, rows]
        if i == n - 1:
            near = near + ref[n + 1, rows]
        side = (lane_full < sh) | (lane_full >= n2 - sh)
        near = near + jnp.where(side, halo(ws, i, p), 0.0)
        low = near[0:8] + jnp.where(row8 < sh, RX[f, 0, i : i + 1], 0.0)
        high = near[n1 - 8 : n1] + jnp.where(row8 >= 8 - sh, RX[f, 1, i : i + 1], 0.0)
        return jnp.concatenate([low, near[8 : n1 - 8], high], axis=0)

    def field(f):
        if f < 3:
            return S.at[f], n0
        return {FGI: (FG, n0), V1I: (V1, m0), V2I: (V2, m0)}[f]

    def message(f, a, d):
        if a == 0:
            if f >= F0I:
                src, dst = F.at[f - F0I, 0], F.at[f - F0I, n0]
            else:
                ref, n = field(f)
                src = ref.at[n if d else 1, rows]
                dst = ref.at[0 if d else n + 1, rows]
        elif a == 1:
            count = m0 if f in (V1I, V2I) else n0
            src, dst = SX.at[f, d, pl.ds(0, count)], RX.at[f, 1 - d, pl.ds(0, count)]
        else:
            src, dst = SY.at[f], RY.at[f, 1 - d]
        step = 1 if d else -1
        return pltpu.make_async_remote_copy(
            src_ref=src, dst_ref=dst, send_sem=send_sem.at[f, a, d], recv_sem=recv_sem.at[f, a, d],
            device_id={AXES[a]: lax.rem(me[a] + step + sizes[a], sizes[a])}, device_id_type=MESH,
        )

    def dirs(f):
        return (0,) if f >= F0I else (0, 1)

    def can_send(a, d):
        return me[a] < sizes[a] - 1 if d else me[a] > 0

    def send(f, a):
        for d in dirs(f):
            pl.when(can_send(a, d))(lambda f=f, a=a, d=d: message(f, a, d).start())

    def receive(f, a):
        for d in dirs(f):
            pl.when(can_send(a, 1 - d))(lambda f=f, a=a, d=d: message(f, a, d).wait_recv())

    def faces_x(f, get, count):
        for i in range(count):
            SX[f, 0, i : i + 1] = get(i, 0)
            if f < F0I:
                SX[f, 1, i : i + 1] = get(i, n1 - 1)

    def rows_x(f, width):
        ref, count = field(f)
        for i in range(count):
            for w in range(width):
                ref[1 + i, PAD - 1 - w : PAD - w] = RX[f, 0, i : i + 1]
                ref[1 + i, PAD + n1 + w : PAD + n1 + w + 1] = RX[f, 1, i : i + 1]

    def exchange(f, p):
        ref, count = field(f)
        send(f, 0)
        faces_x(f, lambda i, r: ref[1 + i, PAD + r : PAD + r + 1], count)
        send(f, 1)
        pack(f, lambda i: ref[1 + i, rows], count, p)
        send(f, 2)

    def one(f, a):
        ref, count = field(f)
        if a == 1:
            faces_x(f, lambda i, r: ref[1 + i, PAD + r : PAD + r + 1], count)
        if a == 2:
            pack(f, lambda i: ref[1 + i, rows], count, 2)
        send(f, a)

    for pos, (k, a) in enumerate(((1, 1), (2, 2), (0, 0))):
        loads[2 * pos].wait()
        loads[2 * pos + 1].wait()
        for i in range(n0):
            inv = 1.0 / D[k, i]
            D[k, i] = inv
            S[k, 1 + i, rows] = R[k, i] * inv
        if pos == 0:
            pl.semaphore_wait(barrier, total)
        one(k, a)
    for f, a in ((0, 1), (2, 1), (1, 0), (2, 0), (0, 2), (1, 2)):
        one(f, a)

    loads[6].wait()
    for i in range(n0):
        NI[i] = 1.0 / (6.0 + NI[i])
    loads[7].wait()
    spread_rows = (
        lax.broadcasted_iota(jnp.int32, (n1, m1), 0) // 2 == lax.broadcasted_iota(jnp.int32, (n1, m1), 1)
    ).astype(jnp.float32)
    spread_cols = (
        lax.broadcasted_iota(jnp.int32, (m2, n2), 1) // 2 == lax.broadcasted_iota(jnp.int32, (m2, n2), 0)
    ).astype(jnp.float32)
    exact = functools.partial(
        jnp.dot, precision=lax.Precision.HIGHEST, preferred_element_type=jnp.float32
    )
    for i in range(m0):
        CI[i] = exact(spread_rows, exact(1.0 / (6.0 + CS[i]), spread_cols))

    for i in range(n0):
        x1, x2 = S[1, 1 + i, rows], S[2, 1 + i, rows]
        rhs = jnp.where(row_full >= 1, S[1, 1 + i, pl.ds(PAD - 1, n1)], 0.0) - x1
        rhs = rhs + (jnp.where(lane_full >= 1, pltpu.roll(x2, 1, 1), 0.0) - x2)
        rhs = rhs - S[0, 1 + i, rows]
        if i > 0:
            rhs = rhs + S[0, i, rows]
        F[0, i] = rhs
    receive(1, 1)
    receive(0, 0)
    receive(2, 2)
    ws = edges(2, 2)
    for i in range(n0):
        rhs = F[0, i] + jnp.where(lane_full < 1, halo(ws, i, 2), 0.0)
        if i == 0:
            rhs = rhs + S[0, 0, rows]
        first = rhs[0:8] + jnp.where(row8 < 1, RX[1, 0, i : i + 1], 0.0)
        FG[1 + i, rows] = jnp.concatenate([first, rhs[8:]], axis=0) * NI[i]
    exchange(FGI, 2)

    def smooth(k):
        for a in range(3):
            if (k, a) not in ((1, 1), (0, 0), (2, 2)):
                receive(k, a)
        rows_x(k, 1)
        w = arrived(k, 2)
        for i in range(n0):
            x = S[k, 1 + i, rows]
            near = S[k, i, rows] + S[k, i + 2, rows] + inplane(S.at[k, 1 + i], x, halo(w, i, 2), 1)
            OB[k, i] = x + near * D[k, i]

    for i in range(n0):
        F[0, i] = local_near(FG, i, n0, 1)
    smooth(0)

    for a in range(3):
        receive(FGI, a)
    ws = edges(FGI, 2)
    for c in range(m0):
        t = None
        for i in (2 * c, 2 * c + 1):
            near = outer_near(F[0, i], FG, FGI, ws, i, n0, 2)
            F[0, i] = near
            t = near if t is None else t + near
        t = t + jnp.where(lane_full % 2 == 0, pltpu.roll(t, n2 - 1, 1), pltpu.roll(t, 1, 1))
        T[c, rows] = t
        t = t + jnp.where(row_full % 2 == 0, T[c, pl.ds(PAD + 1, n1)], T[c, pl.ds(PAD - 1, n1)])
        CR[c] = t
        V1[1 + c, rows] = t * CI[c]
    exchange(V1I, 4)
    for c in range(m0):
        A1[c] = local_near(V1, c, m0, 2)

    def faces_f(j):
        f = F0I + j
        send(f, 0)
        faces_x(f, lambda i, r: F[j, i, r : r + 1], n0)
        send(f, 1)
        pack(f, lambda i: F[j, i], n0, 2)
        send(f, 2)

    for i in range(n0):
        F[0, i] = FG[1 + i, rows] + F[0, i] * NI[i]
    faces_f(0)
    smooth(1)

    for a in range(3):
        receive(V1I, a)
    ws = edges(V1I, 4)
    for c in range(m0):
        near = outer_near(A1[c], V1, V1I, ws, c, m0, 4)
        A1[c] = CR[c] - near
        V2[1 + c, rows] = V1[1 + c, rows] - near * CI[c]
    exchange(V2I, 4)

    def fold(x):
        acc = x[0:8]
        for g in range(1, groups):
            acc = acc + x[8 * g : 8 * g + 8]
        return acc

    def spread_near(j, V, w):
        for c in range(m0):
            x = V[1 + c, rows]
            near = x + inplane(V.at[1 + c], x, halo(w, c, 4), 1)
            F[j, 2 * c] = (near + V[c, rows]) * NI[2 * c]
            F[j, 2 * c + 1] = (near + V[c + 2, rows]) * NI[2 * c + 1]
        faces_f(j)

    sums = [jnp.zeros((8, n2), jnp.float32) for _ in range(5)]
    for c in range(m0):
        v1, v2, a1, cr = V1[1 + c, rows], V2[1 + c, rows], A1[c], CR[c]
        sums[0] = sums[0] + fold(v1 * cr)
        sums[1] = sums[1] + fold(v2 * cr)
        sums[2] = sums[2] + fold(v1 * a1)
        sums[3] = sums[3] + fold(v2 * a1)
        sums[4] = sums[4] + fold(v2 * (a1 - local_near(V2, c, m0, 2)))
    rows_x(V1I, 2)
    spread_near(1, V1, arrived(V1I, 4))

    for a in range(3):
        receive(V2I, a)
    outer = fold(V2[1, rows] * V2[0, rows] + V2[m0, rows] * V2[m0 + 1, rows])
    for v, w in enumerate(edges(V2I, 4)):
        outer = outer + SY[V2I, v] * w
    rim = SX[V2I, 0, 0:m0] * RX[V2I, 0, 0:m0] + SX[V2I, 1, 0:m0] * RX[V2I, 1, 0:m0]
    sums[4] = sums[4] - outer
    rim = 2.0 * jnp.sum(rim, axis=0, keepdims=True)
    sums[4] = sums[4] - jnp.where(row8 == 0, rim, 0.0)
    part = jnp.concatenate(
        [jnp.sum(s, axis=0, keepdims=True) for s in sums] + [jnp.zeros((3, n2), jnp.float32)], axis=0
    )

    def slot(axes, at):
        index = 0
        for a in axes:
            index = index * sizes[a] + at(a)
        return index

    def sum_message(p, offs, sign):
        axes, slots = PHASES[p], (PA, PB)[p]
        other = partner(axes, offs, sign)
        index = slot(axes, (lambda a: me[a]) if sign > 0 else (lambda a: other[AXES[a]]))
        sem = p * PA.shape[0] + slot(axes, lambda a: offs[axes.index(a)])
        return pltpu.make_async_remote_copy(
            src_ref=slots.at[index], dst_ref=slots.at[index], send_sem=psend.at[sem], recv_sem=precv.at[sem],
            device_id=other, device_id_type=MESH,
        )

    def sum_start(p, value):
        (PA, PB)[p][slot(PHASES[p], lambda a: me[a])] = value
        for offs in offsets(PHASES[p]):
            sum_message(p, offs, 1).start()

    def sum_end(p):
        for offs in offsets(PHASES[p]):
            sum_message(p, offs, -1).wait_recv()
        slots = (PA, PB)[p]
        return functools.reduce(lambda x, y: x + y, [slots[d] for d in range(slots.shape[0])])

    sum_start(0, part)
    rows_x(V2I, 2)
    spread_near(2, V2, arrived(V2I, 4))
    smooth(2)
    part = sum_end(0)
    sum_start(1, part)
    for j in range(3):
        for a in range(3):
            receive(F0I + j, a)
    part = sum_end(1)
    tot = jnp.sum(part, axis=1, keepdims=True)
    gone, gtwo, hone, hmix, htwo = [tot[q : q + 1] for q in range(5)]
    two = (gtwo - hmix * gone / hone) / (htwo - hmix * hmix / hone)
    oneco = (gone - hmix * two) / hone

    def mix(get):
        a = get(0)
        return a + jnp.broadcast_to(oneco, a.shape) * get(1) + jnp.broadcast_to(two, a.shape) * get(2)

    for i in range(n0 + 1):
        FN[i, 0:n1] = mix(lambda j: F[j, i])
    for i in range(n0):
        FN[i, n1 : n1 + 1] = mix(lambda j: RX[F0I + j, 1, i : i + 1])
    wf = [mix(lambda j: RY[F0I + j, 1, v]) for v in range(RY.shape[2])]
    for i in range(n0):
        x = FN[i, 0:n1]
        OB[0, i] = OB[0, i] + (FN[i + 1, 0:n1] - x)
        OB[1, i] = OB[1, i] + (FN[i, 1 : n1 + 1] - x)
        OB[2, i] = OB[2, i] + (from_high(x, halo(wf, i, 2)) - x)

    for p in (0, 1):
        for offs in offsets(PHASES[p]):
            sum_message(p, offs, 1).wait_send()
    for a in range(3):
        for d in (0, 1):
            def drain(a=a, d=d):
                for f in range(9):
                    if d in dirs(f):
                        message(f, a, d).wait_send()
            pl.when(can_send(a, d))(drain)


def solution(mesh):
    sizes = tuple(mesh.shape[a] for a in AXES)

    def local(residual, edge_diag, node_shift, coarse_shift):
        n0, n1, n2 = node_shift.shape
        m0, m1, m2 = coarse_shift.shape
        vecs = max(-(-(n0 * (n1 // 8)) // (n2 // 2)), -(-(m0 * (n1 // 8)) // (n2 // 4)))
        f32 = jnp.float32
        counts = [math.prod(sizes[a] for a in axes) for axes in PHASES]
        V = lambda *s: pltpu.VMEM(s, f32)
        scratch = [
            V(3, n0, n1, n2), V(3, n0, n1, n2), V(n0, n1, n2), V(m0, m1, m2),
            V(3, n0 + 2, n1 + 2 * PAD, n2), V(n0 + 2, n1 + 2 * PAD, n2),
            V(m0, n1, n2), V(m0, n1, n2), V(m0, n1, n2), V(m0, n1 + 2 * PAD, n2),
            V(m0 + 2, n1 + 2 * PAD, n2), V(m0 + 2, n1 + 2 * PAD, n2),
            V(3, n0 + 1, n1, n2), V(n0 + 1, n1 + PAD, n2),
            V(9, 2, n0, n2), V(9, 2, n0, n2), V(9, vecs, 8, n2), V(9, 2, vecs, 8, n2),
            *[V(c, 8, n2) for c in counts],
            pltpu.SemaphoreType.DMA((8,)),
            pltpu.SemaphoreType.DMA((9, 3, 2)), pltpu.SemaphoreType.DMA((9, 3, 2)),
            pltpu.SemaphoreType.DMA((sum(counts),)), pltpu.SemaphoreType.DMA((sum(counts),)),
        ]
        limit = 67_043_328 - 4 * math.prod(residual.shape) - 2**16
        return pl.pallas_call(
            functools.partial(kernel, sizes),
            out_shape=pltpu.VMEM(residual.shape, f32),
            in_specs=[pl.BlockSpec(memory_space=pltpu.HBM)] * 4,
            out_specs=pl.BlockSpec(memory_space=pltpu.VMEM),
            scratch_shapes=scratch,
            compiler_params=pltpu.CompilerParams(collective_id=0, has_side_effects=True, vmem_limit_bytes=limit),
        )(residual, edge_diag, node_shift, coarse_shift)

    placed = (
        P(None, "gz", "gx", "gy"),
        P(None, "gz", "gx", "gy"),
        P("gz", "gx", "gy"),
        P("gz", "gx", "gy"),
    )
    return jax.shard_map(
        local, mesh=mesh, in_specs=placed, out_specs=P(None, "gz", "gx", "gy"), check_vma=False
    )
```

profile of v0, /device:TPU:1, one launch (start us, length us, event | category | flops | bytes accessed | tf_op | source)
XLA Modules:
  0.0 27.8 jit_solution(6827979562007463765)
XLA Ops:
  0.0 26.6 %shard_map.46 = f32[3,16,64,128]{3,2,1,0:T(8,128)S(1)} custom-call(f32[3,16,64,128]{3,2,1,0:T(8,128)} %res.1, f32[3,16,64,128]{3,2,1,0:T(8,128)} %dia.1, f32[16,64,128]{2,1,0:T(8,128)} %shf.1, f32[8,32,64]{2,1,0:T(8,128)} %csh.1), custom_call_target="tpu_custom_call" | custom-call | tf_op jit(solution)/shard_map/pallas_call | solution.py:446
  26.7 1.1 %copy.6 = f32[3,16,64,128]{3,2,1,0:T(8,128)} copy(f32[3,16,64,128]{3,2,1,0:T(8,128)S(1)} %shard_map.46) | data formatting | bytes 3145728
where the time goes:
time: 27.9 us; the launch traced here: 27.8 us
  Pallas kernels  26.6 us (95%)
  local copies, waits for them, and re-layouts  1.15 us (4%)
    pallas_call x1, Pallas kernels, local(): pl.pallas_call(functools.partial(kernel, sizes), out_shape=pltpu.VMEM(res...  26.6 us
    unnamed x1, local copies, waits for them, and re-layouts  1.15 us

commit v1 on v0

--- a/solution.py
+++ b/solution.py
@@ -13,16 +13,34 @@
 AXES = ("gz", "gx", "gy")
 FGI, V1I, V2I, F0I = 3, 4, 5, 6
 PAD = 8
-PHASES = ((1, 2), (0,))
+FEW = 32
+
+
+def phases_of(sizes):
+    return ((0, 1, 2),) if math.prod(sizes) <= FEW else ((1, 2), (0,))
+
+
+def greeted(sizes, rounds, moves):
+    near = set(itertools.product((-1, 0, 1), repeat=3))
+    known = set(near)
+    for _ in range(rounds):
+        known |= {tuple(p + q for p, q in zip(k, m)) for k in known for m in moves}
+    needed = set()
+    for axes in phases_of(sizes):
+        spans = [range(1 - sizes[a], sizes[a]) if a in axes else (0,) for a in range(3)]
+        needed |= set(itertools.product(*spans))
+    every = near | (needed - known)
+    return sorted(o for o in every if any(o) and all(abs(p) < n for p, n in zip(o, sizes)))
 
 
 def kernel(
     sizes,
-    res, dia, shf, csh, OB,
-    R, D, NI, CS, S, FG, CI, CR, A1, T, V1, V2, F, FN,
-    SX, RX, SY, RY, PA, PB,
-    in_sem, send_sem, recv_sem, psend, precv,
+    res, dia, shf, csh, OB, G1, G2, CO,
+    R, D, NI, CS, S, FG, CI, CR, A1, T, V1, V2, F,
+    SX, RX, SY, RY,
+    in_sem, send_sem, recv_sem, psend, precv, *slots_of,
 ):
+    phases = phases_of(sizes)
     n0, n1, n2 = NI.shape
     m0, m1, m2 = CS.shape
     groups = n1 // 8
@@ -51,7 +69,7 @@
     for k in range(3):
         S[k, 0, rows] = zplane
         S[k, n0 + 1, rows] = zplane
-        F[k, n0] = zplane
+        F[k, n0, 0:n1] = zplane
     FG[0, rows] = zplane
     FG[n0 + 1, rows] = zplane
     for V in (V1, V2):
@@ -60,11 +78,17 @@
     RX[...] = jnp.zeros(RX.shape, jnp.float32)
     RY[...] = jnp.zeros(RY.shape, jnp.float32)
     barrier = pltpu.get_barrier_semaphore()
-    total = 0
-    for axes in PHASES:
-        for offs in offsets(axes):
-            pl.semaphore_signal(barrier, inc=1, device_id=partner(axes, offs, 1), device_id_type=MESH)
-            total += 1
+    faces = [tuple(d if b == a else 0 for b in range(3)) for a in range(3) for d in (-1, 1)]
+    total = jnp.int32(0)
+    for offs in greeted(sizes, 4, faces):
+        there = functools.reduce(
+            jnp.logical_and, [(me[a] + o >= 0) & (me[a] + o < sizes[a]) for a, o in enumerate(offs) if o]
+        )
+        peer = {AXES[a]: me[a] + o for a, o in enumerate(offs) if o}
+        pl.when(there)(
+            lambda peer=peer: pl.semaphore_signal(barrier, inc=1, device_id=peer, device_id_type=MESH)
+        )
+        total = total + there.astype(jnp.int32)
 
     lane = lax.broadcasted_iota(jnp.int32, (8, n2), 1)
     lane_full = lax.broadcasted_iota(jnp.int32, (n1, n2), 1)
@@ -150,7 +174,7 @@
     def message(f, a, d):
         if a == 0:
             if f >= F0I:
-                src, dst = F.at[f - F0I, 0], F.at[f - F0I, n0]
+                src, dst = F.at[f - F0I, 0, pl.ds(0, n1)], F.at[f - F0I, n0, pl.ds(0, n1)]
             else:
                 ref, n = field(f)
                 src = ref.at[n if d else 1, rows]
@@ -245,13 +269,13 @@
         rhs = rhs - S[0, 1 + i, rows]
         if i > 0:
             rhs = rhs + S[0, i, rows]
-        F[0, i] = rhs
+        F[0, i, 0:n1] = rhs
     receive(1, 1)
     receive(0, 0)
     receive(2, 2)
     ws = edges(2, 2)
     for i in range(n0):
-        rhs = F[0, i] + jnp.where(lane_full < 1, halo(ws, i, 2), 0.0)
+        rhs = F[0, i, 0:n1] + jnp.where(lane_full < 1, halo(ws, i, 2), 0.0)
         if i == 0:
             rhs = rhs + S[0, 0, rows]
         first = rhs[0:8] + jnp.where(row8 < 1, RX[1, 0, i : i + 1], 0.0)
@@ -270,7 +294,7 @@
             OB[k, i] = x + near * D[k, i]
 
     for i in range(n0):
-        F[0, i] = local_near(FG, i, n0, 1)
+        F[0, i, 0:n1] = local_near(FG, i, n0, 1)
     smooth(0)
 
     for a in range(3):
@@ -279,8 +303,8 @@
     for c in range(m0):
         t = None
         for i in (2 * c, 2 * c + 1):
-            near = outer_near(F[0, i], FG, FGI, ws, i, n0, 2)
-            F[0, i] = near
+            near = outer_near(F[0, i, 0:n1], FG, FGI, ws, i, n0, 2)
+            F[0, i, 0:n1] = near
             t = near if t is None else t + near
         t = t + jnp.where(lane_full % 2 == 0, pltpu.roll(t, n2 - 1, 1), pltpu.roll(t, 1, 1))
         T[c, rows] = t
@@ -296,11 +320,11 @@
         send(f, 0)
         faces_x(f, lambda i, r: F[j, i, r : r + 1], n0)
         send(f, 1)
-        pack(f, lambda i: F[j, i], n0, 2)
+        pack(f, lambda i: F[j, i, 0:n1], n0, 2)
         send(f, 2)
 
     for i in range(n0):
-        F[0, i] = FG[1 + i, rows] + F[0, i] * NI[i]
+        F[0, i, 0:n1] = FG[1 + i, rows] + F[0, i, 0:n1] * NI[i]
     faces_f(0)
     smooth(1)
 
@@ -323,8 +347,8 @@
         for c in range(m0):
             x = V[1 + c, rows]
             near = x + inplane(V.at[1 + c], x, halo(w, c, 4), 1)
-            F[j, 2 * c] = (near + V[c, rows]) * NI[2 * c]
-            F[j, 2 * c + 1] = (near + V[c + 2, rows]) * NI[2 * c + 1]
+            F[j, 2 * c, 0:n1] = (near + V[c, rows]) * NI[2 * c]
+            F[j, 2 * c + 1, 0:n1] = (near + V[c + 2, rows]) * NI[2 * c + 1]
         faces_f(j)
 
     sums = [jnp.zeros((8, n2), jnp.float32) for _ in range(5)]
@@ -347,9 +371,10 @@
     sums[4] = sums[4] - outer
     rim = 2.0 * jnp.sum(rim, axis=0, keepdims=True)
     sums[4] = sums[4] - jnp.where(row8 == 0, rim, 0.0)
-    part = jnp.concatenate(
-        [jnp.sum(s, axis=0, keepdims=True) for s in sums] + [jnp.zeros((3, n2), jnp.float32)], axis=0
-    )
+    lane1 = lax.broadcasted_iota(jnp.int32, (1, n2), 1)
+    part = jnp.zeros((1, n2), jnp.float32)
+    for q, s in enumerate(sums):
+        part = jnp.where(lane1 == q, jnp.sum(jnp.sum(s, axis=0, keepdims=True), axis=1, keepdims=True), part)
 
     def slot(axes, at):
         index = 0
@@ -358,58 +383,58 @@
         return index
 
     def sum_message(p, offs, sign):
-        axes, slots = PHASES[p], (PA, PB)[p]
+        axes, slots = phases[p], slots_of[p]
         other = partner(axes, offs, sign)
         index = slot(axes, (lambda a: me[a]) if sign > 0 else (lambda a: other[AXES[a]]))
-        sem = p * PA.shape[0] + slot(axes, lambda a: offs[axes.index(a)])
+        sem = p * slots_of[0].shape[0] + slot(axes, lambda a: offs[axes.index(a)])
         return pltpu.make_async_remote_copy(
             src_ref=slots.at[index], dst_ref=slots.at[index], send_sem=psend.at[sem], recv_sem=precv.at[sem],
             device_id=other, device_id_type=MESH,
         )
 
     def sum_start(p, value):
-        (PA, PB)[p][slot(PHASES[p], lambda a: me[a])] = value
-        for offs in offsets(PHASES[p]):
+        slots_of[p][slot(phases[p], lambda a: me[a])] = value
+        for offs in offsets(phases[p]):
             sum_message(p, offs, 1).start()
 
     def sum_end(p):
-        for offs in offsets(PHASES[p]):
+        for offs in offsets(phases[p]):
             sum_message(p, offs, -1).wait_recv()
-        slots = (PA, PB)[p]
-        return functools.reduce(lambda x, y: x + y, [slots[d] for d in range(slots.shape[0])])
+        terms = [slots_of[p][d] for d in range(slots_of[p].shape[0])]
+        while len(terms) > 1:
+            terms = [functools.reduce(lambda x, y: x + y, terms[t : t + 2]) for t in range(0, len(terms), 2)]
+        return terms[0]
 
     sum_start(0, part)
     rows_x(V2I, 2)
     spread_near(2, V2, arrived(V2I, 4))
     smooth(2)
-    part = sum_end(0)
-    sum_start(1, part)
-    for j in range(3):
+    for j, G in enumerate((OB, G1, G2)):
         for a in range(3):
             receive(F0I + j, a)
-    part = sum_end(1)
-    tot = jnp.sum(part, axis=1, keepdims=True)
-    gone, gtwo, hone, hmix, htwo = [tot[q : q + 1] for q in range(5)]
+        for i in range(n0):
+            F[j, i, n1 : n1 + 1] = RX[F0I + j, 1, i : i + 1]
+        wf = [RY[F0I + j, 1, v] for v in range(RY.shape[2])]
+        for i in range(n0):
+            x = F[j, i, 0:n1]
+            grads = (F[j, i + 1, 0:n1] - x, F[j, i, 1 : n1 + 1] - x, from_high(x, halo(wf, i, 2)) - x)
+            for k in range(3):
+                G[k, i] = G[k, i] + grads[k] if j == 0 else grads[k]
+
+    part = sum_end(0)
+    for p in range(1, len(phases)):
+        sum_start(p, part)
+        part = sum_end(p)
+    gone, gtwo, hone, hmix, htwo = [
+        jnp.sum(jnp.where(lane1 == q, part, 0.0), axis=1, keepdims=True) for q in range(5)
+    ]
     two = (gtwo - hmix * gone / hone) / (htwo - hmix * hmix / hone)
     oneco = (gone - hmix * two) / hone
-
-    def mix(get):
-        a = get(0)
-        return a + jnp.broadcast_to(oneco, a.shape) * get(1) + jnp.broadcast_to(two, a.shape) * get(2)
-
-    for i in range(n0 + 1):
-        FN[i, 0:n1] = mix(lambda j: F[j, i])
-    for i in range(n0):
-        FN[i, n1 : n1 + 1] = mix(lambda j: RX[F0I + j, 1, i : i + 1])
-    wf = [mix(lambda j: RY[F0I + j, 1, v]) for v in range(RY.shape[2])]
-    for i in range(n0):
-        x = FN[i, 0:n1]
-        OB[0, i] = OB[0, i] + (FN[i + 1, 0:n1] - x)
-        OB[1, i] = OB[1, i] + (FN[i, 1 : n1 + 1] - x)
-        OB[2, i] = OB[2, i] + (from_high(x, halo(wf, i, 2)) - x)
-
-    for p in (0, 1):
-        for offs in offsets(PHASES[p]):
+    CO[0:1] = jnp.broadcast_to(oneco, (1, n2))
+    CO[1:2] = jnp.broadcast_to(two, (1, n2))
+
+    for p in range(len(phases)):
+        for offs in offsets(phases[p]):
             sum_message(p, offs, 1).wait_send()
     for a in range(3):
         for d in (0, 1):
@@ -420,6 +445,23 @@
             pl.when(can_send(a, d))(drain)
 
 
+def combine(parts, OB, G1, G2, CO, out, W, sem):
+    _, n0, n1, n2 = OB.shape
+    one = jnp.broadcast_to(CO[0:1], (n1, n2))
+    two = jnp.broadcast_to(CO[1:2], (n1, n2))
+    step = n0 // parts
+    copies = []
+    for k in range(3):
+        for h in range(parts):
+            for i in range(h * step, (h + 1) * step):
+                W[k, i] = OB[k, i] + one * G1[k, i] + two * G2[k, i]
+            planes = pl.ds(h * step, step)
+            copies.append(pltpu.make_async_copy(W.at[k, planes], out.at[k, planes], sem.at[k * parts + h]))
+            copies[-1].start()
+    for c in copies:
+        c.wait()
+
+
 def solution(mesh):
     sizes = tuple(mesh.shape[a] for a in AXES)
 
@@ -428,29 +470,39 @@
         m0, m1, m2 = coarse_shift.shape
         vecs = max(-(-(n0 * (n1 // 8)) // (n2 // 2)), -(-(m0 * (n1 // 8)) // (n2 // 4)))
         f32 = jnp.float32
-        counts = [math.prod(sizes[a] for a in axes) for axes in PHASES]
+        counts = [math.prod(sizes[a] for a in axes) for axes in phases_of(sizes)]
         V = lambda *s: pltpu.VMEM(s, f32)
         scratch = [
             V(3, n0, n1, n2), V(3, n0, n1, n2), V(n0, n1, n2), V(m0, m1, m2),
             V(3, n0 + 2, n1 + 2 * PAD, n2), V(n0 + 2, n1 + 2 * PAD, n2),
             V(m0, n1, n2), V(m0, n1, n2), V(m0, n1, n2), V(m0, n1 + 2 * PAD, n2),
             V(m0 + 2, n1 + 2 * PAD, n2), V(m0 + 2, n1 + 2 * PAD, n2),
-            V(3, n0 + 1, n1, n2), V(n0 + 1, n1 + PAD, n2),
+            V(3, n0 + 1, n1 + PAD, n2),
             V(9, 2, n0, n2), V(9, 2, n0, n2), V(9, vecs, 8, n2), V(9, 2, vecs, 8, n2),
-            *[V(c, 8, n2) for c in counts],
             pltpu.SemaphoreType.DMA((8,)),
             pltpu.SemaphoreType.DMA((9, 3, 2)), pltpu.SemaphoreType.DMA((9, 3, 2)),
             pltpu.SemaphoreType.DMA((sum(counts),)), pltpu.SemaphoreType.DMA((sum(counts),)),
+            *[V(c, 1, n2) for c in counts],
         ]
-        limit = 67_043_328 - 4 * math.prod(residual.shape) - 2**16
-        return pl.pallas_call(
+        field = pltpu.VMEM(residual.shape, f32)
+        limit = 67_043_328 - 12 * math.prod(residual.shape) - 2**18
+        fields = pl.pallas_call(
             functools.partial(kernel, sizes),
-            out_shape=pltpu.VMEM(residual.shape, f32),
+            out_shape=[field, field, field, pltpu.VMEM((8, n2), f32)],
             in_specs=[pl.BlockSpec(memory_space=pltpu.HBM)] * 4,
-            out_specs=pl.BlockSpec(memory_space=pltpu.VMEM),
+            out_specs=[pl.BlockSpec(memory_space=pltpu.VMEM)] * 4,
             scratch_shapes=scratch,
             compiler_params=pltpu.CompilerParams(collective_id=0, has_side_effects=True, vmem_limit_bytes=limit),
         )(residual, edge_diag, node_shift, coarse_shift)
+        parts = 2 if n0 % 2 == 0 else 1
+        return pl.pallas_call(
+            functools.partial(combine, parts),
+            out_shape=jax.ShapeDtypeStruct(residual.shape, f32),
+            in_specs=[pl.BlockSpec(memory_space=pltpu.VMEM)] * 4,
+            out_specs=pl.BlockSpec(memory_space=pltpu.HBM),
+            scratch_shapes=[field, pltpu.SemaphoreType.DMA((3 * parts,))],
+            compiler_params=pltpu.CompilerParams(vmem_limit_bytes=8 * math.prod(residual.shape)),
+        )(*fields)
 
     placed = (
         P(None, "gz", "gx", "gy"),

time: 27.9 us -> 26.6 us (0.953)
  the two profiles are of different devices: /device:TPU:1 before, /device:TPU:0 now
where the time goes in v1:
time: 26.6 us; the launch traced here: 26.4 us
  Pallas kernels  26.4 us (99%)
    pallas_call x1, Pallas kernels, local(): pl.pallas_call(functools.partial(kernel, sizes), out_shape=[field, field,...  25.2 us
    pallas_call x1, Pallas kernels, local(): pl.pallas_call(functools.partial(combine, parts), out_shape=jax.ShapeDtyp...  1.23 us

profile of v1, /device:TPU:0, one launch (start us, length us, event | category | flops | bytes accessed | tf_op | source)
XLA Modules:
  0.0 26.4 jit_solution(4994964831931665329)
XLA Ops:
  0.0 25.2 %shard_map.46 = (f32[3,16,64,128]{3,2,1,0:T(8,128)S(1)}, f32[3,16,64,128]{3,2,1,0:T(8,128)S(1)}, f32[3,16,64,128]{3,2,1,0:T(8,128)S(1)}, f32[8,128]{1,0:T(8,128)S(1)}) custom-call(f32[3,16,64,128]{3,2,1,0:T(8,128)} %res.1, f32[3,16,64,128]{3,2,1,0:T(8,128)} %dia.1, f32[16,64,128]{2,1,0:T(8,128)} %shf.1, f32[8,32,64]{2,1,0:T(8,128)} %csh.1), custom_call_target="tpu_custom_call" | custom-call | tf_op jit(solution)/shard_map/pallas_call | solution.py:489
  25.2 1.2 %shard_map.47 = f32[3,16,64,128]{3,2,1,0:T(8,128)} custom-call(f32[3,16,64,128]{3,2,1,0:T(8,128)S(1)} %get-tuple-element.9.OB, f32[3,16,64,128]{3,2,1,0:T(8,128)S(1)} %get-tuple-element.10.G1, f32[3,16,64,128]{3,2,1,0:T(8,128)S(1)} %get-tuple-element.11.G2, f32[8,128]{1,0:T(8,128)S(1)} %get-tuple-element.12.CO), custom_call_target="tpu_custom_call" | custom-call | tf_op jit(solution)/shard_map/pallas_call | solution.py:498

commit v2 on v1

--- a/solution.py
+++ b/solution.py
@@ -38,7 +38,8 @@
     res, dia, shf, csh, OB, G1, G2, CO,
     R, D, NI, CS, S, FG, CI, CR, A1, T, V1, V2, F,
     SX, RX, SY, RY,
-    in_sem, send_sem, recv_sem, psend, precv, *slots_of,
+    slots_of,
+    in_sem, send_sem, recv_sem, psend, precv,
 ):
     phases = phases_of(sizes)
     n0, n1, n2 = NI.shape
@@ -479,15 +480,18 @@
             V(m0 + 2, n1 + 2 * PAD, n2), V(m0 + 2, n1 + 2 * PAD, n2),
             V(3, n0 + 1, n1 + PAD, n2),
             V(9, 2, n0, n2), V(9, 2, n0, n2), V(9, vecs, 8, n2), V(9, 2, vecs, 8, n2),
-            pltpu.SemaphoreType.DMA((8,)),
-            pltpu.SemaphoreType.DMA((9, 3, 2)), pltpu.SemaphoreType.DMA((9, 3, 2)),
-            pltpu.SemaphoreType.DMA((sum(counts),)), pltpu.SemaphoreType.DMA((sum(counts),)),
             *[V(c, 1, n2) for c in counts],
         ]
+        sems = [pltpu.SemaphoreType.DMA(s) for s in ((8,), (9, 3, 2), (9, 3, 2), (sum(counts),), (sum(counts),))]
+
+        def scoped(*refs):
+            plain, slots_of = refs[: -len(counts)], refs[-len(counts) :]
+            pl.run_scoped(functools.partial(kernel, sizes, *plain, slots_of), *sems)
+
         field = pltpu.VMEM(residual.shape, f32)
         limit = 67_043_328 - 12 * math.prod(residual.shape) - 2**18
         fields = pl.pallas_call(
-            functools.partial(kernel, sizes),
+            scoped,
             out_shape=[field, field, field, pltpu.VMEM((8, n2), f32)],
             in_specs=[pl.BlockSpec(memory_space=pltpu.HBM)] * 4,
             out_specs=[pl.BlockSpec(memory_space=pltpu.VMEM)] * 4,

time: 26.6 us -> 24.9 us (0.936)
  Pallas kernels: 26.4 us -> 24.8 us
    pallas_call x1, Pallas kernels: 25.2 us -> 23.6 us  [local(): pl.pallas_call(scoped, out_shape=[field, field, field, pltpu.VMEM((8, n2)...]
where the time goes in v2:
time: 24.9 us; the launch traced here: 24.8 us
  Pallas kernels  24.8 us (100%)
    pallas_call x1, Pallas kernels, local(): pl.pallas_call(scoped, out_shape=[field, field, field, pltpu.VMEM((8, n2)...  23.6 us
    pallas_call x1, Pallas kernels, local(): pl.pallas_call(functools.partial(combine, parts), out_shape=jax.ShapeDtyp...  1.23 us

profile of v2, /device:TPU:0, one launch (start us, length us, event | category | flops | bytes accessed | tf_op | source)
XLA Modules:
  0.0 24.8 jit_solution(2371212102573032705)
XLA Ops:
  0.0 23.6 %shard_map.46 = (f32[3,16,64,128]{3,2,1,0:T(8,128)S(1)}, f32[3,16,64,128]{3,2,1,0:T(8,128)S(1)}, f32[3,16,64,128]{3,2,1,0:T(8,128)S(1)}, f32[8,128]{1,0:T(8,128)S(1)}) custom-call(f32[3,16,64,128]{3,2,1,0:T(8,128)} %refs_0_.1, f32[3,16,64,128]{3,2,1,0:T(8,128)} %refs_1_.1, f32[16,64,128]{2,1,0:T(8,128)} %refs_2_.1, f32[8,32,64]{2,1,0:T(8,128)} %refs_3_.1), custom_call_target="tpu_custom_call" | custom-call | tf_op jit(solution)/shard_map/pallas_call | solution.py:493
  23.6 1.2 %shard_map.47 = f32[3,16,64,128]{3,2,1,0:T(8,128)} custom-call(f32[3,16,64,128]{3,2,1,0:T(8,128)S(1)} %get-tuple-element.9.OB, f32[3,16,64,128]{3,2,1,0:T(8,128)S(1)} %get-tuple-element.10.G1, f32[3,16,64,128]{3,2,1,0:T(8,128)S(1)} %get-tuple-element.11.G2, f32[8,128]{1,0:T(8,128)S(1)} %get-tuple-element.12.CO), custom_call_target="tpu_custom_call" | custom-call | tf_op jit(solution)/shard_map/pallas_call | solution.py:502

commit v3 on v2

--- a/solution.py
+++ b/solution.py
@@ -11,7 +11,10 @@
 
 MESH = pl.DeviceIdType.MESH
 AXES = ("gz", "gx", "gy")
-FGI, V1I, V2I, F0I = 3, 4, 5, 6
+FGI, V1I, V2I, F0I, NLI, CII = 3, 4, 5, 6, 9, 10
+FIELDS = 11
+FINAL = (F0I, F0I + 1, F0I + 2)
+COARSE = (V1I, V2I, NLI, CII)
 PAD = 8
 FEW = 32
 
@@ -20,10 +23,10 @@
     return ((0, 1, 2),) if math.prod(sizes) <= FEW else ((1, 2), (0,))
 
 
-def greeted(sizes, rounds, moves):
+def greeted(sizes, rounds):
     near = set(itertools.product((-1, 0, 1), repeat=3))
     known = set(near)
-    for _ in range(rounds):
+    for moves in rounds:
         known |= {tuple(p + q for p, q in zip(k, m)) for k in known for m in moves}
     needed = set()
     for axes in phases_of(sizes):
@@ -36,10 +39,10 @@
 def kernel(
     sizes,
     res, dia, shf, csh, OB, G1, G2, CO,
-    R, D, NI, CS, S, FG, CI, CR, A1, T, V1, V2, F,
-    SX, RX, SY, RY,
+    R, D, NI, CS, S, FG, CI, CR, A1, NL, T, V1, V2, F,
+    SX, RX, SY, RY, NZ, CZ, LZX, LXY, RZX, RZY, RXY,
     slots_of,
-    in_sem, send_sem, recv_sem, psend, precv,
+    in_sem, send_sem, recv_sem, psend, precv, lsend, lrecv,
 ):
     phases = phases_of(sizes)
     n0, n1, n2 = NI.shape
@@ -76,18 +79,26 @@
     for V in (V1, V2):
         V[0, rows] = zplane
         V[m0 + 1, rows] = zplane
-    RX[...] = jnp.zeros(RX.shape, jnp.float32)
-    RY[...] = jnp.zeros(RY.shape, jnp.float32)
+    for buf in (RX, RY, NZ, CZ, RZX, RZY, RXY):
+        buf[...] = jnp.zeros(buf.shape, jnp.float32)
     barrier = pltpu.get_barrier_semaphore()
-    faces = [tuple(d if b == a else 0 for b in range(3)) for a in range(3) for d in (-1, 1)]
+    faces = [offs for offs in itertools.product((-1, 0, 1), repeat=3) if sum(map(abs, offs)) == 1]
+    lines = [offs for offs in itertools.product((-1, 0, 1), repeat=3) if sum(map(abs, offs)) == 2]
+
+    def exists(offs):
+        inside = [(me[a] + o >= 0) & (me[a] + o < sizes[a]) for a, o in enumerate(offs) if o]
+        return functools.reduce(jnp.logical_and, inside)
+
+    def device(offs):
+        return {AXES[a]: me[a] + o for a, o in enumerate(offs) if o}
+
     total = jnp.int32(0)
-    for offs in greeted(sizes, 4, faces):
-        there = functools.reduce(
-            jnp.logical_and, [(me[a] + o >= 0) & (me[a] + o < sizes[a]) for a, o in enumerate(offs) if o]
-        )
-        peer = {AXES[a]: me[a] + o for a, o in enumerate(offs) if o}
+    for offs in greeted(sizes, (faces, faces, faces + lines)):
+        there = exists(offs)
         pl.when(there)(
-            lambda peer=peer: pl.semaphore_signal(barrier, inc=1, device_id=peer, device_id_type=MESH)
+            lambda offs=offs: pl.semaphore_signal(
+                barrier, inc=1, device_id=device(offs), device_id_type=MESH
+            )
         )
         total = total + there.astype(jnp.int32)
 
@@ -136,6 +147,11 @@
         near = ref[pl.ds(PAD - sh, n1)] + ref[pl.ds(PAD + sh, n1)]
         return near + from_low(x, h, sh) + from_high(x, h, sh)
 
+    def inplane_aligned(ref, x, h, sh):
+        near = ref[pl.ds(PAD - sh, n1)] + ref[pl.ds(PAD + sh, n1)]
+        near = near + jnp.where(lane_full < sh, h, pltpu.roll(x, sh, 1))
+        return near + jnp.where(lane_full >= n2 - sh, h, pltpu.roll(x, n2 - sh, 1))
+
     def local_near(ref, i, n, sh):
         x = ref[1 + i, rows]
         near = jnp.where(row_full >= sh, ref[1 + i, pl.ds(PAD - sh, n1)], 0.0)
@@ -170,18 +186,21 @@
     def field(f):
         if f < 3:
             return S.at[f], n0
-        return {FGI: (FG, n0), V1I: (V1, m0), V2I: (V2, m0)}[f]
+        return {FGI: (FG, n0), V1I: (V1, m0)}[f]
 
     def message(f, a, d):
         if a == 0:
-            if f >= F0I:
+            if f in FINAL:
                 src, dst = F.at[f - F0I, 0, pl.ds(0, n1)], F.at[f - F0I, n0, pl.ds(0, n1)]
+            elif f in (NLI, CII):
+                src, dst = {NLI: (NL, NZ), CII: (CI, CZ)}[f]
+                src, dst = src.at[m0 - 1 if d else 0], dst.at[1 - d]
             else:
                 ref, n = field(f)
                 src = ref.at[n if d else 1, rows]
                 dst = ref.at[0 if d else n + 1, rows]
         elif a == 1:
-            count = m0 if f in (V1I, V2I) else n0
+            count = m0 if f in COARSE else n0
             src, dst = SX.at[f, d, pl.ds(0, count)], RX.at[f, 1 - d, pl.ds(0, count)]
         else:
             src, dst = SY.at[f], RY.at[f, 1 - d]
@@ -192,7 +211,7 @@
         )
 
     def dirs(f):
-        return (0,) if f >= F0I else (0, 1)
+        return (0,) if f in FINAL else (0, 1)
 
     def can_send(a, d):
         return me[a] < sizes[a] - 1 if d else me[a] > 0
@@ -208,15 +227,99 @@
     def faces_x(f, get, count):
         for i in range(count):
             SX[f, 0, i : i + 1] = get(i, 0)
-            if f < F0I:
+            if f not in FINAL:
                 SX[f, 1, i : i + 1] = get(i, n1 - 1)
 
-    def rows_x(f, width):
-        ref, count = field(f)
-        for i in range(count):
+    def rows_x(f, ref):
+        width = 2 if f in COARSE else 1
+        for i in range(m0 if f in COARSE else n0):
             for w in range(width):
                 ref[1 + i, PAD - 1 - w : PAD - w] = RX[f, 0, i : i + 1]
                 ref[1 + i, PAD + n1 + w : PAD + n1 + w + 1] = RX[f, 1, i : i + 1]
+
+    def line_message(offs, sign):
+        z, x, y = [o * sign for o in offs]
+        side = [0 if o > 0 else 1 for o in (z, x, y)]
+        if not y:
+            src, dst = LZX.at[1 - side[0], 1 - side[1]], RZX.at[side[0], side[1]]
+        elif not x:
+            plane = place(m0 - 1 if z > 0 else 0, 0, 4)[0]
+            src, dst = SY.at[V1I, plane], RZY.at[side[0], side[2]]
+        else:
+            src, dst = LXY.at[1 - side[1]], RXY.at[side[1], side[2]]
+        at = lines.index((z, x, y))
+        return pltpu.make_async_remote_copy(
+            src_ref=src, dst_ref=dst, send_sem=lsend.at[at], recv_sem=lrecv.at[at],
+            device_id=device((z, x, y)), device_id_type=MESH,
+        )
+
+    def lines_send():
+        for z in (0, 1):
+            for x in (0, 1):
+                c, r = (m0 - 1) * z, (n1 - 1) * x
+                LZX[z, x] = V1[1 + c, PAD + r : PAD + r + 1]
+        for x in (0, 1):
+            for v in range(LXY.shape[1]):
+                LXY[x, v] = SY[V1I, v, 7 * x : 7 * x + 1]
+        for offs in lines:
+            pl.when(exists(offs))(lambda offs=offs: line_message(offs, 1).start())
+
+    def lines_receive():
+        for offs in lines:
+            pl.when(exists(offs))(lambda offs=offs: line_message(offs, -1).wait_recv())
+
+    def align(low, high, p):
+        return jnp.where(is_low[p], pltpu.roll(high, n2 - p // 2, 1), pltpu.roll(low, p // 2, 1))
+
+    def halo_v2(ev, enl, eci):
+        sh, kgroup = 2, [place(c, 0, 4) for c in (m0 - 1, 0)]
+        col = [align(RZY[d, 0], RZY[d, 1], 4) for d in (0, 1)]
+        for d, edge in ((0, 0), (1, m0 + 1)):
+            v, kk = kgroup[d]
+            near = NZ[d] + V1[1 if d == 0 else m0, rows]
+            parts = [pltpu.roll(col[d], (n2 - 4 * (kk + g)) % n2, 1) for g in range(groups)]
+            side = (lane_full < sh) | (lane_full >= n2 - sh)
+            near = near + jnp.where(side, jnp.concatenate(parts, axis=0), 0.0)
+            low = near[0:8] + jnp.where(row8 < sh, RZX[d, 0], 0.0)
+            high = near[n1 - 8 : n1] + jnp.where(row8 >= 8 - sh, RZX[d, 1], 0.0)
+            near = jnp.concatenate([low, near[8 : n1 - 8], high], axis=0)
+            V2[edge, rows] = V1[edge, rows] - CZ[d] * near
+        rowc = lax.broadcasted_iota(jnp.int32, (m0, n2), 0)
+        lanec = lax.broadcasted_iota(jnp.int32, (m0, n2), 1)
+        per = n2 // 4
+        for d in (0, 1):
+            near = RX[NLI, d, 0:m0] + SX[V1I, d, 0:m0]
+            near = near + jnp.where(rowc == 0, RZX[0, d], 0.0) + jnp.where(rowc == m0 - 1, RZX[1, d], 0.0)
+            for y in (0, 1):
+                index = rowc * groups + (groups - 1 if d == 0 else 0)
+                at = lax.rem(4 * lax.rem(index, per) + (n2 - 1 if y == 0 else 0), n2)
+                got = jnp.zeros((m0, n2), jnp.float32)
+                for v in range(RXY.shape[2]):
+                    here = (lanec == at) & (index >= v * per) & (index < (v + 1) * per)
+                    got = got + jnp.where(here, RXY[d, y, v], 0.0)
+                got = jnp.sum(got, axis=1, keepdims=True)
+                near = near + jnp.where((lanec < sh) if y == 0 else (lanec >= n2 - sh), got, 0.0)
+            RX[V2I, d, 0:m0] = RX[V1I, d, 0:m0] - RX[CII, d, 0:m0] * near
+        ws = []
+        for v in range(len(ev)):
+            near = enl[v] + SY[V1I, v]
+            for d, c in ((0, 0), (1, m0 - 1)):
+                into, k0 = place(c, 0, 4)
+                if into == v:
+                    shift = (4 * (k0 - kgroup[d][1])) % n2
+                    moved = pltpu.roll(col[d], shift, 1) if shift else col[d]
+                    near = near + jnp.where((keys[4] >= k0) & (keys[4] < k0 + groups), moved, 0.0)
+            for d in (0, 1):
+                line = align(
+                    jnp.broadcast_to(RXY[d, 0, v], (8, n2)), jnp.broadcast_to(RXY[d, 1, v], (8, n2)), 4
+                )
+                jump = 4 * (groups - 1)
+                line = pltpu.roll(line, n2 - jump if d == 0 else jump, 1)
+                here = lax.rem(keys[4], groups) == (0 if d == 0 else groups - 1)
+                here = here & ((row8 < sh) if d == 0 else (row8 >= 8 - sh))
+                near = near + jnp.where(here, line, 0.0)
+            ws.append(ev[v] - eci[v] * near)
+        return ws
 
     def exchange(f, p):
         ref, count = field(f)
@@ -233,6 +336,13 @@
         if a == 2:
             pack(f, lambda i: ref[1 + i, rows], count, 2)
         send(f, a)
+
+    def spread_faces(f, ref):
+        send(f, 0)
+        faces_x(f, lambda c, r: ref[c, r : r + 1], m0)
+        send(f, 1)
+        pack(f, lambda c: ref[c], m0, 4)
+        send(f, 2)
 
     for pos, (k, a) in enumerate(((1, 1), (2, 2), (0, 0))):
         loads[2 * pos].wait()
@@ -262,6 +372,7 @@
     )
     for i in range(m0):
         CI[i] = exact(spread_rows, exact(1.0 / (6.0 + CS[i]), spread_cols))
+    spread_faces(CII, CI)
 
     for i in range(n0):
         x1, x2 = S[1, 1 + i, rows], S[2, 1 + i, rows]
@@ -287,7 +398,7 @@
         for a in range(3):
             if (k, a) not in ((1, 1), (0, 0), (2, 2)):
                 receive(k, a)
-        rows_x(k, 1)
+        rows_x(k, S.at[k])
         w = arrived(k, 2)
         for i in range(n0):
             x = S[k, 1 + i, rows]
@@ -297,6 +408,7 @@
     for i in range(n0):
         F[0, i, 0:n1] = local_near(FG, i, n0, 1)
     smooth(0)
+    smooth(1)
 
     for a in range(3):
         receive(FGI, a)
@@ -313,8 +425,10 @@
         CR[c] = t
         V1[1 + c, rows] = t * CI[c]
     exchange(V1I, 4)
+    lines_send()
     for c in range(m0):
-        A1[c] = local_near(V1, c, m0, 2)
+        NL[c] = local_near(V1, c, m0, 2)
+    spread_faces(NLI, NL)
 
     def faces_f(j):
         f = F0I + j
@@ -327,16 +441,20 @@
     for i in range(n0):
         F[0, i, 0:n1] = FG[1 + i, rows] + F[0, i, 0:n1] * NI[i]
     faces_f(0)
-    smooth(1)
-
-    for a in range(3):
-        receive(V1I, a)
+    smooth(2)
+
+    for f in (CII, V1I, NLI):
+        for a in range(3):
+            receive(f, a)
     ws = edges(V1I, 4)
     for c in range(m0):
-        near = outer_near(A1[c], V1, V1I, ws, c, m0, 4)
+        near = outer_near(NL[c], V1, V1I, ws, c, m0, 4)
         A1[c] = CR[c] - near
         V2[1 + c, rows] = V1[1 + c, rows] - near * CI[c]
-    exchange(V2I, 4)
+    faces_x(V2I, lambda c, r: V2[1 + c, PAD + r : PAD + r + 1], m0)
+    pack(V2I, lambda c: V2[1 + c, rows], m0, 4)
+    lines_receive()
+    w2 = halo_v2(ws, edges(NLI, 4), edges(CII, 4))
 
     def fold(x):
         acc = x[0:8]
@@ -347,7 +465,7 @@
     def spread_near(j, V, w):
         for c in range(m0):
             x = V[1 + c, rows]
-            near = x + inplane(V.at[1 + c], x, halo(w, c, 4), 1)
+            near = x + inplane_aligned(V.at[1 + c], x, halo(w, c, 4), 1)
             F[j, 2 * c, 0:n1] = (near + V[c, rows]) * NI[2 * c]
             F[j, 2 * c + 1, 0:n1] = (near + V[c + 2, rows]) * NI[2 * c + 1]
         faces_f(j)
@@ -360,13 +478,8 @@
         sums[2] = sums[2] + fold(v1 * a1)
         sums[3] = sums[3] + fold(v2 * a1)
         sums[4] = sums[4] + fold(v2 * (a1 - local_near(V2, c, m0, 2)))
-    rows_x(V1I, 2)
-    spread_near(1, V1, arrived(V1I, 4))
-
-    for a in range(3):
-        receive(V2I, a)
     outer = fold(V2[1, rows] * V2[0, rows] + V2[m0, rows] * V2[m0 + 1, rows])
-    for v, w in enumerate(edges(V2I, 4)):
+    for v, w in enumerate(w2):
         outer = outer + SY[V2I, v] * w
     rim = SX[V2I, 0, 0:m0] * RX[V2I, 0, 0:m0] + SX[V2I, 1, 0:m0] * RX[V2I, 1, 0:m0]
     sums[4] = sums[4] - outer
@@ -407,9 +520,10 @@
         return terms[0]
 
     sum_start(0, part)
-    rows_x(V2I, 2)
-    spread_near(2, V2, arrived(V2I, 4))
-    smooth(2)
+    rows_x(V2I, V2)
+    spread_near(2, V2, w2)
+    rows_x(V1I, V1)
+    spread_near(1, V1, ws)
     for j, G in enumerate((OB, G1, G2)):
         for a in range(3):
             receive(F0I + j, a)
@@ -437,11 +551,13 @@
     for p in range(len(phases)):
         for offs in offsets(phases[p]):
             sum_message(p, offs, 1).wait_send()
+    for offs in lines:
+        pl.when(exists(offs))(lambda offs=offs: line_message(offs, 1).wait_send())
     for a in range(3):
         for d in (0, 1):
             def drain(a=a, d=d):
-                for f in range(9):
-                    if d in dirs(f):
+                for f in range(FIELDS):
+                    if f != V2I and d in dirs(f):
                         message(f, a, d).wait_send()
             pl.when(can_send(a, d))(drain)
 
@@ -476,13 +592,15 @@
         scratch = [
             V(3, n0, n1, n2), V(3, n0, n1, n2), V(n0, n1, n2), V(m0, m1, m2),
             V(3, n0 + 2, n1 + 2 * PAD, n2), V(n0 + 2, n1 + 2 * PAD, n2),
-            V(m0, n1, n2), V(m0, n1, n2), V(m0, n1, n2), V(m0, n1 + 2 * PAD, n2),
+            V(m0, n1, n2), V(m0, n1, n2), V(m0, n1, n2), V(m0, n1, n2), V(m0, n1 + 2 * PAD, n2),
             V(m0 + 2, n1 + 2 * PAD, n2), V(m0 + 2, n1 + 2 * PAD, n2),
             V(3, n0 + 1, n1 + PAD, n2),
-            V(9, 2, n0, n2), V(9, 2, n0, n2), V(9, vecs, 8, n2), V(9, 2, vecs, 8, n2),
+            V(FIELDS, 2, n0, n2), V(FIELDS, 2, n0, n2), V(FIELDS, vecs, 8, n2), V(FIELDS, 2, vecs, 8, n2),
+            V(2, n1, n2), V(2, n1, n2), V(2, 2, 1, n2), V(2, vecs, 1, n2),
+            V(2, 2, 1, n2), V(2, 2, 8, n2), V(2, 2, vecs, 1, n2),
             *[V(c, 1, n2) for c in counts],
         ]
-        sems = [pltpu.SemaphoreType.DMA(s) for s in ((8,), (9, 3, 2), (9, 3, 2), (sum(counts),), (sum(counts),))]
+        sems = [pltpu.SemaphoreType.DMA(s) for s in ((8,), *[(FIELDS, 3, 2)] * 2, *[(sum(counts),)] * 2, (12,), (12,))]
 
         def scoped(*refs):
             plain, slots_of = refs[: -len(counts)], refs[-len(counts) :]

time: 24.9 us -> 23.9 us (0.960)
  Pallas kernels: 24.8 us -> 23.7 us
    pallas_call x1, Pallas kernels: 23.6 us -> 22.5 us  [local(): pl.pallas_call(scoped, out_shape=[field, field, field, pltpu.VMEM((8, n2)...]
where the time goes in v3:
time: 23.9 us; the launch traced here: 23.7 us
  Pallas kernels  23.7 us (99%)
    pallas_call x1, Pallas kernels, local(): pl.pallas_call(scoped, out_shape=[field, field, field, pltpu.VMEM((8, n2)...  22.5 us
    pallas_call x1, Pallas kernels, local(): pl.pallas_call(functools.partial(combine, parts), out_shape=jax.ShapeDtyp...  1.23 us

profile of v3, /device:TPU:0, one launch (start us, length us, event | category | flops | bytes accessed | tf_op | source)
XLA Modules:
  0.0 23.7 jit_solution(4688928367331535155)
XLA Ops:
  0.0 22.5 %shard_map.46 = (f32[3,16,64,128]{3,2,1,0:T(8,128)S(1)}, f32[3,16,64,128]{3,2,1,0:T(8,128)S(1)}, f32[3,16,64,128]{3,2,1,0:T(8,128)S(1)}, f32[8,128]{1,0:T(8,128)S(1)}) custom-call(f32[3,16,64,128]{3,2,1,0:T(8,128)} %refs_0_.1, f32[3,16,64,128]{3,2,1,0:T(8,128)} %refs_1_.1, f32[16,64,128]{2,1,0:T(8,128)} %refs_2_.1, f32[8,32,64]{2,1,0:T(8,128)} %refs_3_.1), custom_call_target="tpu_custom_call" | custom-call | tf_op jit(solution)/shard_map/pallas_call | solution.py:611
  22.5 1.2 %shard_map.47 = f32[3,16,64,128]{3,2,1,0:T(8,128)} custom-call(f32[3,16,64,128]{3,2,1,0:T(8,128)S(1)} %get-tuple-element.9.OB, f32[3,16,64,128]{3,2,1,0:T(8,128)S(1)} %get-tuple-element.10.G1, f32[3,16,64,128]{3,2,1,0:T(8,128)S(1)} %get-tuple-element.11.G2, f32[8,128]{1,0:T(8,128)S(1)} %get-tuple-element.12.CO), custom_call_target="tpu_custom_call" | custom-call | tf_op jit(solution)/shard_map/pallas_call | solution.py:620

commit v4 on v3

--- a/solution.py
+++ b/solution.py
@@ -38,7 +38,7 @@
 
 def kernel(
     sizes,
-    res, dia, shf, csh, OB, G1, G2, CO,
+    res, dia, shf, csh, OB, G1, G2, CO, MZ, MX, MY,
     R, D, NI, CS, S, FG, CI, CR, A1, NL, T, V1, V2, F,
     SX, RX, SY, RY, NZ, CZ, LZX, LXY, RZX, RZY, RXY,
     slots_of,
@@ -74,6 +74,8 @@
         S[k, 0, rows] = zplane
         S[k, n0 + 1, rows] = zplane
         F[k, n0, 0:n1] = zplane
+        for i in range(n0):
+            F[k, i, n1 : n1 + 1] = jnp.zeros((1, n2), jnp.float32)
     FG[0, rows] = zplane
     FG[n0 + 1, rows] = zplane
     for V in (V1, V2):
@@ -127,9 +129,6 @@
         for v, acc in enumerate(accs):
             SY[f, v] = acc
 
-    def arrived(f, p):
-        return [jnp.where(is_low[p], RY[f, 0, v], RY[f, 1, v]) for v in range(RY.shape[2])]
-
     def halo(ws, i, p):
         parts = []
         for g in range(groups):
@@ -137,17 +136,7 @@
             parts.append(pltpu.roll(ws[v], n2 - p * kk, 1) if kk else ws[v])
         return jnp.concatenate(parts, axis=0)
 
-    def from_low(x, h, sh=1):
-        return pltpu.roll(jnp.where(lane_full >= n2 - sh, h, x), sh, 1)
-
-    def from_high(x, h, sh=1):
-        return pltpu.roll(jnp.where(lane_full < sh, h, x), n2 - sh, 1)
-
     def inplane(ref, x, h, sh):
-        near = ref[pl.ds(PAD - sh, n1)] + ref[pl.ds(PAD + sh, n1)]
-        return near + from_low(x, h, sh) + from_high(x, h, sh)
-
-    def inplane_aligned(ref, x, h, sh):
         near = ref[pl.ds(PAD - sh, n1)] + ref[pl.ds(PAD + sh, n1)]
         near = near + jnp.where(lane_full < sh, h, pltpu.roll(x, sh, 1))
         return near + jnp.where(lane_full >= n2 - sh, h, pltpu.roll(x, n2 - sh, 1))
@@ -392,6 +381,14 @@
             rhs = rhs + S[0, 0, rows]
         first = rhs[0:8] + jnp.where(row8 < 1, RX[1, 0, i : i + 1], 0.0)
         FG[1 + i, rows] = jnp.concatenate([first, rhs[8:]], axis=0) * NI[i]
+    def gradients(j, G):
+        for i in range(n0):
+            x = F[j, i, 0:n1]
+            above = F[j, i + 1, 0:n1] - x if i < n0 - 1 else -x
+            ahead = jnp.where(lane_full >= n2 - 1, 0.0, pltpu.roll(x, n2 - 1, 1)) - x
+            for k, grad in enumerate((above, F[j, i, 1 : n1 + 1] - x, ahead)):
+                G[k, i] = G[k, i] + grad if j == 0 else grad
+
     exchange(FGI, 2)
 
     def smooth(k):
@@ -399,7 +396,7 @@
             if (k, a) not in ((1, 1), (0, 0), (2, 2)):
                 receive(k, a)
         rows_x(k, S.at[k])
-        w = arrived(k, 2)
+        w = edges(k, 2)
         for i in range(n0):
             x = S[k, 1 + i, rows]
             near = S[k, i, rows] + S[k, i + 2, rows] + inplane(S.at[k, 1 + i], x, halo(w, i, 2), 1)
@@ -442,6 +439,7 @@
         F[0, i, 0:n1] = FG[1 + i, rows] + F[0, i, 0:n1] * NI[i]
     faces_f(0)
     smooth(2)
+    gradients(0, OB)
 
     for f in (CII, V1I, NLI):
         for a in range(3):
@@ -465,7 +463,7 @@
     def spread_near(j, V, w):
         for c in range(m0):
             x = V[1 + c, rows]
-            near = x + inplane_aligned(V.at[1 + c], x, halo(w, c, 4), 1)
+            near = x + inplane(V.at[1 + c], x, halo(w, c, 4), 1)
             F[j, 2 * c, 0:n1] = (near + V[c, rows]) * NI[2 * c]
             F[j, 2 * c + 1, 0:n1] = (near + V[c + 2, rows]) * NI[2 * c + 1]
         faces_f(j)
@@ -524,17 +522,8 @@
     spread_near(2, V2, w2)
     rows_x(V1I, V1)
     spread_near(1, V1, ws)
-    for j, G in enumerate((OB, G1, G2)):
-        for a in range(3):
-            receive(F0I + j, a)
-        for i in range(n0):
-            F[j, i, n1 : n1 + 1] = RX[F0I + j, 1, i : i + 1]
-        wf = [RY[F0I + j, 1, v] for v in range(RY.shape[2])]
-        for i in range(n0):
-            x = F[j, i, 0:n1]
-            grads = (F[j, i + 1, 0:n1] - x, F[j, i, 1 : n1 + 1] - x, from_high(x, halo(wf, i, 2)) - x)
-            for k in range(3):
-                G[k, i] = G[k, i] + grads[k] if j == 0 else grads[k]
+    gradients(1, G1)
+    gradients(2, G2)
 
     part = sum_end(0)
     for p in range(1, len(phases)):
@@ -547,6 +536,18 @@
     oneco = (gone - hmix * two) / hone
     CO[0:1] = jnp.broadcast_to(oneco, (1, n2))
     CO[1:2] = jnp.broadcast_to(two, (1, n2))
+    for f in FINAL:
+        for a in range(3):
+            receive(f, a)
+
+    def mix(get):
+        a = get(0)
+        return a + jnp.broadcast_to(oneco, a.shape) * get(1) + jnp.broadcast_to(two, a.shape) * get(2)
+
+    MZ[...] = mix(lambda j: F[j, n0, 0:n1])
+    MX[...] = mix(lambda j: RX[F0I + j, 1])
+    for v in range(RY.shape[2]):
+        MY[v] = pltpu.roll(mix(lambda j: RY[F0I + j, 1, v]), n2 - 1, 1)
 
     for p in range(len(phases)):
         for offs in offsets(phases[p]):
@@ -562,16 +563,29 @@
             pl.when(can_send(a, d))(drain)
 
 
-def combine(parts, OB, G1, G2, CO, out, W, sem):
+def combine(parts, OB, G1, G2, CO, MZ, MX, MY, out, W, sem):
     _, n0, n1, n2 = OB.shape
     one = jnp.broadcast_to(CO[0:1], (n1, n2))
     two = jnp.broadcast_to(CO[1:2], (n1, n2))
-    step = n0 // parts
+    groups, per, step = n1 // 8, n2 // 2, n0 // parts
+    row8 = lax.broadcasted_iota(jnp.int32, (8, n2), 0)
+    lane_full = lax.broadcasted_iota(jnp.int32, (n1, n2), 1)
+
+    def edge(k, i, x):
+        if k == 0:
+            return x + MZ[...] if i == n0 - 1 else x
+        if k == 1:
+            last = x[n1 - 8 : n1] + jnp.where(row8 == 7, MX[i : i + 1], 0.0)
+            return jnp.concatenate([x[0 : n1 - 8], last], axis=0)
+        ats = [divmod(i * groups + g, per) for g in range(groups)]
+        parts = [pltpu.roll(MY[v], (n2 - 2 * kk) % n2, 1) for v, kk in ats]
+        return x + jnp.where(lane_full >= n2 - 1, jnp.concatenate(parts, axis=0), 0.0)
+
     copies = []
     for k in range(3):
         for h in range(parts):
             for i in range(h * step, (h + 1) * step):
-                W[k, i] = OB[k, i] + one * G1[k, i] + two * G2[k, i]
+                W[k, i] = edge(k, i, OB[k, i] + one * G1[k, i] + two * G2[k, i])
             planes = pl.ds(h * step, step)
             copies.append(pltpu.make_async_copy(W.at[k, planes], out.at[k, planes], sem.at[k * parts + h]))
             copies[-1].start()
@@ -610,9 +624,9 @@
         limit = 67_043_328 - 12 * math.prod(residual.shape) - 2**18
         fields = pl.pallas_call(
             scoped,
-            out_shape=[field, field, field, pltpu.VMEM((8, n2), f32)],
+            out_shape=[field] * 3 + [pltpu.VMEM(s, f32) for s in ((8, n2), (n1, n2), (n0, n2), (vecs, 8, n2))],
             in_specs=[pl.BlockSpec(memory_space=pltpu.HBM)] * 4,
-            out_specs=[pl.BlockSpec(memory_space=pltpu.VMEM)] * 4,
+            out_specs=[pl.BlockSpec(memory_space=pltpu.VMEM)] * 7,
             scratch_shapes=scratch,
             compiler_params=pltpu.CompilerParams(collective_id=0, has_side_effects=True, vmem_limit_bytes=limit),
         )(residual, edge_diag, node_shift, coarse_shift)
@@ -620,7 +634,7 @@
         return pl.pallas_call(
             functools.partial(combine, parts),
             out_shape=jax.ShapeDtypeStruct(residual.shape, f32),
-            in_specs=[pl.BlockSpec(memory_space=pltpu.VMEM)] * 4,
+            in_specs=[pl.BlockSpec(memory_space=pltpu.VMEM)] * 7,
             out_specs=pl.BlockSpec(memory_space=pltpu.HBM),
             scratch_shapes=[field, pltpu.SemaphoreType.DMA((3 * parts,))],
             compiler_params=pltpu.CompilerParams(vmem_limit_bytes=8 * math.prod(residual.shape)),

time: 23.9 us -> 22.9 us (0.958)
  Pallas kernels: 23.7 us -> 22.8 us
    pallas_call x1, Pallas kernels: 22.5 us -> 21.6 us  [local(): pl.pallas_call(scoped, out_shape=[field] * 3 + [pltpu.VMEM(s, f32) for s...]
where the time goes in v4:
time: 22.9 us; the launch traced here: 22.8 us
  Pallas kernels  22.8 us (100%)
    pallas_call x1, Pallas kernels, local(): pl.pallas_call(scoped, out_shape=[field] * 3 + [pltpu.VMEM(s, f32) for s...  21.6 us
    pallas_call x1, Pallas kernels, local(): pl.pallas_call(functools.partial(combine, parts), out_shape=jax.ShapeDtyp...  1.23 us

profile of v4, /device:TPU:0, one launch (start us, length us, event | category | flops | bytes accessed | tf_op | source)
XLA Modules:
  0.0 22.8 jit_solution(6090050886919487469)
XLA Ops:
  0.0 21.6 %shard_map.46 = (f32[3,16,64,128]{3,2,1,0:T(8,128)S(1)}, f32[3,16,64,128]{3,2,1,0:T(8,128)S(1)}, f32[3,16,64,128]{3,2,1,0:T(8,128)S(1)}, f32[8,128]{1,0:T(8,128)...) custom-call(f32[3,16,64,128]{3,2,1,0:T(8,128)} %refs_0_.1, ...), custom_call_target="tpu_custom_call" | custom-call | tf_op jit(solution)/shard_map/pallas_call | solution.py:625
  21.6 1.2 %shard_map.47 = f32[3,16,64,128]{3,2,1,0:T(8,128)} custom-call(f32[3,16,64,128]{3,2,1,0:T(8,128)S(1)} %get-tuple-element.12.OB, f32[3,16,64,128]{3,2,1,0:T(8,128)S(1)} %get-tuple-element.13.G1, f32[3,16,64,128]{3,2,1,0:T(8,128)S(1)} %get-tuple-element.14.G2, f32[8,128]{1,0:T(8,128)S(1)} %get-tuple-element.15.CO, f32[64,128]{1,0:T(8,128)S(1)} %get-tuple-element.16.MZ, ...), custom_call_target="tpu_custom_call" | custom-call | tf_op jit(solution)/shard_map/pallas_call | solution.py:634

commit v5 on v4

--- a/solution.py
+++ b/solution.py
@@ -11,10 +11,12 @@
 
 MESH = pl.DeviceIdType.MESH
 AXES = ("gz", "gx", "gy")
-FGI, V1I, V2I, F0I, NLI, CII = 3, 4, 5, 6, 9, 10
-FIELDS = 11
+PI, V1I, V2I, F0I, NLI, CII, NII, FGI = 3, 4, 5, 6, 9, 10, 11, 12
+FIELDS = 13
 FINAL = (F0I, F0I + 1, F0I + 2)
 COARSE = (V1I, V2I, NLI, CII)
+LOCAL = (V2I, FGI)
+CROSS = [(a, b, d) for a in range(3) for b in range(3) if a != b for d in (0, 1)]
 PAD = 8
 FEW = 32
 
@@ -24,7 +26,7 @@
 
 
 def greeted(sizes, rounds):
-    near = set(itertools.product((-1, 0, 1), repeat=3))
+    near = set(itertools.product(range(-1, 2), range(-2, 3), range(-2, 3)))
     known = set(near)
     for moves in rounds:
         known |= {tuple(p + q for p, q in zip(k, m)) for k in known for m in moves}
@@ -41,8 +43,9 @@
     res, dia, shf, csh, OB, G1, G2, CO, MZ, MX, MY,
     R, D, NI, CS, S, FG, CI, CR, A1, NL, T, V1, V2, F,
     SX, RX, SY, RY, NZ, CZ, LZX, LXY, RZX, RZY, RXY,
+    P, PZ, NZI, LRZ, LRX, LY2, LY1, LP0, RRZ, RRX, RZ2, RZ0, RX2, RX1,
     slots_of,
-    in_sem, send_sem, recv_sem, psend, precv, lsend, lrecv,
+    in_sem, send_sem, recv_sem, psend, precv, lsend, lrecv, csend, crecv,
 ):
     phases = phases_of(sizes)
     n0, n1, n2 = NI.shape
@@ -60,11 +63,10 @@
             AXES[a]: lax.rem(me[a] + (o if sign > 0 else sizes[a] - o), sizes[a]) for a, o in zip(axes, offs)
         }
 
-    loads = []
+    loads = [pltpu.make_async_copy(shf, NI, in_sem.at[0])]
     for k in (1, 2, 0):
         for src, dst in ((res, R), (dia, D)):
             loads.append(pltpu.make_async_copy(src.at[k], dst.at[k], in_sem.at[len(loads)]))
-    loads.append(pltpu.make_async_copy(shf, NI, in_sem.at[6]))
     loads.append(pltpu.make_async_copy(csh, CS, in_sem.at[7]))
     for c in loads:
         c.start()
@@ -76,12 +78,10 @@
         F[k, n0, 0:n1] = zplane
         for i in range(n0):
             F[k, i, n1 : n1 + 1] = jnp.zeros((1, n2), jnp.float32)
-    FG[0, rows] = zplane
-    FG[n0 + 1, rows] = zplane
     for V in (V1, V2):
         V[0, rows] = zplane
         V[m0 + 1, rows] = zplane
-    for buf in (RX, RY, NZ, CZ, RZX, RZY, RXY):
+    for buf in (RX, RY, NZ, CZ, RZX, RZY, RXY, PZ, NZI, RRZ, RRX, RZ2, RZ0, RX2, RX1):
         buf[...] = jnp.zeros(buf.shape, jnp.float32)
     barrier = pltpu.get_barrier_semaphore()
     faces = [offs for offs in itertools.product((-1, 0, 1), repeat=3) if sum(map(abs, offs)) == 1]
@@ -95,7 +95,7 @@
         return {AXES[a]: me[a] + o for a, o in enumerate(offs) if o}
 
     total = jnp.int32(0)
-    for offs in greeted(sizes, (faces, faces, faces + lines)):
+    for offs in greeted(sizes, (faces + [m for m in lines if min(m) < 0], faces + lines)):
         there = exists(offs)
         pl.when(there)(
             lambda offs=offs: pl.semaphore_signal(
@@ -116,17 +116,20 @@
         per = n2 // p
         return k // per, k % per
 
+    def gather(blocks, p):
+        accs = {}
+        for (i, g), part in blocks:
+            v, kk = place(i, g, p)
+            if kk:
+                part = pltpu.roll(part, p * kk, 1)
+            accs[v] = jnp.where(keys[p] == kk, part, accs.get(v, 0.0))
+        return accs
+
     def pack(f, plane, count, p):
-        accs = [jnp.zeros((8, n2), jnp.float32) for _ in range(place(count - 1, groups - 1, p)[0] + 1)]
-        for i in range(count):
-            x = plane(i)
-            for g in range(groups):
-                v, kk = place(i, g, p)
-                part = x[8 * g : 8 * g + 8]
-                if kk:
-                    part = pltpu.roll(part, p * kk, 1)
-                accs[v] = jnp.where(keys[p] == kk, part, accs[v])
-        for v, acc in enumerate(accs):
+        at = [(i, g) for i in range(count) for g in range(groups)]
+        planes = [plane(i) for i in range(count)]
+        accs = gather([((i, g), planes[i][8 * g : 8 * g + 8]) for i, g in at], p)
+        for v, acc in accs.items():
             SY[f, v] = acc
 
     def halo(ws, i, p):
@@ -175,15 +178,17 @@
     def field(f):
         if f < 3:
             return S.at[f], n0
-        return {FGI: (FG, n0), V1I: (V1, m0)}[f]
+        return {V1I: (V1, m0)}[f]
+
+    ZBUF = {NLI: (NL, NZ, m0), CII: (CI, CZ, m0), PI: (P, PZ, n0), NII: (NI, NZI, n0)}
 
     def message(f, a, d):
         if a == 0:
             if f in FINAL:
                 src, dst = F.at[f - F0I, 0, pl.ds(0, n1)], F.at[f - F0I, n0, pl.ds(0, n1)]
-            elif f in (NLI, CII):
-                src, dst = {NLI: (NL, NZ), CII: (CI, CZ)}[f]
-                src, dst = src.at[m0 - 1 if d else 0], dst.at[1 - d]
+            elif f in ZBUF:
+                src, dst, n = ZBUF[f]
+                src, dst = src.at[n - 1 if d else 0], dst.at[1 - d]
             else:
                 ref, n = field(f)
                 src = ref.at[n if d else 1, rows]
@@ -241,6 +246,83 @@
             src_ref=src, dst_ref=dst, send_sem=lsend.at[at], recv_sem=lrecv.at[at],
             device_id=device((z, x, y)), device_id_type=MESH,
         )
+
+    def cross_message(a, b, d, sign):
+        src, dst = {
+            (0, 1): (LRZ.at[d], RRZ.at[d]),
+            (1, 0): (LRX.at[d], RRX.at[d]),
+            (0, 2): (SY.at[2, place(0 if d else n0 - 1, 0, 2)[0]], RZ2.at[d]),
+            (2, 0): (LP0, RZ0.at[d]),
+            (1, 2): (LY2.at[d], RX2.at[d]),
+            (2, 1): (LY1, RX1.at[d]),
+        }[a, b]
+        at = CROSS.index((a, b, d))
+        return pltpu.make_async_remote_copy(
+            src_ref=src, dst_ref=dst, send_sem=csend.at[at], recv_sem=crecv.at[at],
+            device_id=device(cross_offs(a, b, d, sign)), device_id_type=MESH,
+        )
+
+    def cross_offs(a, b, d, sign):
+        offs = [0, 0, 0]
+        offs[a], offs[b] = (-sign if d else sign), sign
+        return tuple(offs)
+
+    def cross_rows():
+        for d in (0, 1):
+            i, r = (0 if d else n0 - 1), (0 if d else n1 - 1)
+            LRZ[d] = S[1, 1 + i, PAD + n1 - 1 : PAD + n1]
+            LRX[d] = S[0, n0, PAD + r : PAD + r + 1]
+            for v in range(LY2.shape[1]):
+                LY2[d, v] = SY[2, v, (0 if d else 7) : (1 if d else 8)]
+        top = [((n0 - 1, g), S[0, n0, PAD + 8 * g : PAD + 8 * g + 8]) for g in range(groups)]
+        for acc in gather(top, 2).values():
+            LP0[...] = acc
+        last = [((i, groups - 1), S[1, 1 + i, PAD + n1 - 8 : PAD + n1]) for i in range(n0)]
+        for v, acc in gather(last, 2).items():
+            LY1[v] = acc[7:8]
+
+    def cross_send():
+        for at in CROSS:
+            pl.when(exists(cross_offs(*at, 1)))(lambda at=at: cross_message(*at, 1).start())
+
+    def cross_receive():
+        for at in CROSS:
+            pl.when(exists(cross_offs(*at, -1)))(lambda at=at: cross_message(*at, -1).wait_recv())
+
+    def halo_fg():
+        for d in (0, 1):
+            kk = place(0 if d else n0 - 1, 0, 2)[1]
+            rhs = PZ[d] + S[0, n0, rows] if d else PZ[d]
+            col = [pltpu.roll(RZ2[d], (2 * n2 - 2 * (kk + g) + 1) % n2, 1) for g in range(groups)]
+            rhs = rhs + jnp.where(lane_full < 1, jnp.concatenate(col, axis=0), 0.0)
+            first = rhs[0:8] + jnp.where(row8 < 1, RRZ[d], 0.0)
+            FG[(n0 + 1) * d, rows] = jnp.concatenate([first, rhs[8:]], axis=0) * NZI[d]
+        rowi = lax.broadcasted_iota(jnp.int32, (n0, n2), 0)
+        lanei = lax.broadcasted_iota(jnp.int32, (n0, n2), 1)
+        per = n2 // 2
+        for d in (0, 1):
+            rhs = RX[PI, d] + SX[1, 1] if d else RX[PI, d]
+            rhs = rhs + jnp.where(rowi == 0, RRX[d], 0.0)
+            index = rowi * groups + (0 if d else groups - 1)
+            at = lax.rem(2 * lax.rem(index, per) + n2 - 1, n2)
+            got = jnp.zeros((n0, n2), jnp.float32)
+            for v in range(RX2.shape[1]):
+                here = (lanei == at) & (index >= v * per) & (index < (v + 1) * per)
+                got = got + jnp.where(here, RX2[d, v], 0.0)
+            rhs = rhs + jnp.where(lanei < 1, jnp.sum(got, axis=1, keepdims=True), 0.0)
+            RX[FGI, d] = rhs * RX[NII, d]
+        ws = []
+        for v, (ep, en) in enumerate(zip(edges(PI, 2), edges(NII, 2))):
+            rhs = ep + jnp.where(is_low[2], SY[2, v], 0.0)
+            if v == 0:
+                k0 = place(n0 - 1, 0, 2)[1]
+                moved = pltpu.roll(align(RZ0[0], RZ0[1], 2), (n2 - 2 * k0) % n2, 1)
+                rhs = rhs + jnp.where(keys[2] < groups, moved, 0.0)
+            line = align(jnp.broadcast_to(RX1[0, v], (8, n2)), jnp.broadcast_to(RX1[1, v], (8, n2)), 2)
+            line = pltpu.roll(line, n2 - 2 * (groups - 1), 1)
+            here = (lax.rem(keys[2], groups) == 0) & (row8 < 1)
+            ws.append((rhs + jnp.where(here, line, 0.0)) * en)
+        return ws
 
     def lines_send():
         for z in (0, 1):
@@ -326,29 +408,44 @@
             pack(f, lambda i: ref[1 + i, rows], count, 2)
         send(f, a)
 
-    def spread_faces(f, ref):
+    def spread_faces(f, ref, n, p):
         send(f, 0)
-        faces_x(f, lambda c, r: ref[c, r : r + 1], m0)
+        faces_x(f, lambda c, r: ref[c, r : r + 1], n)
         send(f, 1)
-        pack(f, lambda c: ref[c], m0, 4)
+        pack(f, lambda c: ref[c], n, p)
         send(f, 2)
 
+    def partial_rhs():
+        for i in range(n0):
+            x1, x2 = S[1, 1 + i, rows], S[2, 1 + i, rows]
+            rhs = jnp.where(row_full >= 1, S[1, 1 + i, pl.ds(PAD - 1, n1)], 0.0) - x1
+            rhs = rhs + (jnp.where(lane_full >= 1, pltpu.roll(x2, 1, 1), 0.0) - x2)
+            rhs = rhs - S[0, 1 + i, rows]
+            if i > 0:
+                rhs = rhs + S[0, i, rows]
+            P[i] = rhs
+
+    loads[0].wait()
+    for i in range(n0):
+        NI[i] = 1.0 / (6.0 + NI[i])
     for pos, (k, a) in enumerate(((1, 1), (2, 2), (0, 0))):
-        loads[2 * pos].wait()
-        loads[2 * pos + 1].wait()
+        loads[1 + 2 * pos].wait()
+        loads[2 + 2 * pos].wait()
         for i in range(n0):
             inv = 1.0 / D[k, i]
             D[k, i] = inv
             S[k, 1 + i, rows] = R[k, i] * inv
         if pos == 0:
             pl.semaphore_wait(barrier, total)
+            spread_faces(NII, NI, n0, 2)
         one(k, a)
+    partial_rhs()
+    cross_rows()
+    cross_send()
+    spread_faces(PI, P, n0, 2)
     for f, a in ((0, 1), (2, 1), (1, 0), (2, 0), (0, 2), (1, 2)):
         one(f, a)
 
-    loads[6].wait()
-    for i in range(n0):
-        NI[i] = 1.0 / (6.0 + NI[i])
     loads[7].wait()
     spread_rows = (
         lax.broadcasted_iota(jnp.int32, (n1, m1), 0) // 2 == lax.broadcasted_iota(jnp.int32, (n1, m1), 1)
@@ -361,22 +458,14 @@
     )
     for i in range(m0):
         CI[i] = exact(spread_rows, exact(1.0 / (6.0 + CS[i]), spread_cols))
-    spread_faces(CII, CI)
-
-    for i in range(n0):
-        x1, x2 = S[1, 1 + i, rows], S[2, 1 + i, rows]
-        rhs = jnp.where(row_full >= 1, S[1, 1 + i, pl.ds(PAD - 1, n1)], 0.0) - x1
-        rhs = rhs + (jnp.where(lane_full >= 1, pltpu.roll(x2, 1, 1), 0.0) - x2)
-        rhs = rhs - S[0, 1 + i, rows]
-        if i > 0:
-            rhs = rhs + S[0, i, rows]
-        F[0, i, 0:n1] = rhs
+    spread_faces(CII, CI, m0, 4)
+
     receive(1, 1)
     receive(0, 0)
     receive(2, 2)
     ws = edges(2, 2)
     for i in range(n0):
-        rhs = F[0, i, 0:n1] + jnp.where(lane_full < 1, halo(ws, i, 2), 0.0)
+        rhs = P[i] + jnp.where(lane_full < 1, halo(ws, i, 2), 0.0)
         if i == 0:
             rhs = rhs + S[0, 0, rows]
         first = rhs[0:8] + jnp.where(row8 < 1, RX[1, 0, i : i + 1], 0.0)
@@ -389,7 +478,6 @@
             for k, grad in enumerate((above, F[j, i, 1 : n1 + 1] - x, ahead)):
                 G[k, i] = G[k, i] + grad if j == 0 else grad
 
-    exchange(FGI, 2)
 
     def smooth(k):
         for a in range(3):
@@ -404,12 +492,12 @@
 
     for i in range(n0):
         F[0, i, 0:n1] = local_near(FG, i, n0, 1)
-    smooth(0)
-    smooth(1)
-
-    for a in range(3):
-        receive(FGI, a)
-    ws = edges(FGI, 2)
+
+    for f in (NII, PI):
+        for a in range(3):
+            receive(f, a)
+    cross_receive()
+    ws = halo_fg()
     for c in range(m0):
         t = None
         for i in (2 * c, 2 * c + 1):
@@ -425,7 +513,7 @@
     lines_send()
     for c in range(m0):
         NL[c] = local_near(V1, c, m0, 2)
-    spread_faces(NLI, NL)
+    spread_faces(NLI, NL, m0, 4)
 
     def faces_f(j):
         f = F0I + j
@@ -438,7 +526,8 @@
     for i in range(n0):
         F[0, i, 0:n1] = FG[1 + i, rows] + F[0, i, 0:n1] * NI[i]
     faces_f(0)
-    smooth(2)
+    for k in (1, 2, 0):
+        smooth(k)
     gradients(0, OB)
 
     for f in (CII, V1I, NLI):
@@ -554,11 +643,13 @@
             sum_message(p, offs, 1).wait_send()
     for offs in lines:
         pl.when(exists(offs))(lambda offs=offs: line_message(offs, 1).wait_send())
+    for at in CROSS:
+        pl.when(exists(cross_offs(*at, 1)))(lambda at=at: cross_message(*at, 1).wait_send())
     for a in range(3):
         for d in (0, 1):
             def drain(a=a, d=d):
                 for f in range(FIELDS):
-                    if f != V2I and d in dirs(f):
+                    if f not in LOCAL and d in dirs(f):
                         message(f, a, d).wait_send()
             pl.when(can_send(a, d))(drain)
 
@@ -612,9 +703,11 @@
             V(FIELDS, 2, n0, n2), V(FIELDS, 2, n0, n2), V(FIELDS, vecs, 8, n2), V(FIELDS, 2, vecs, 8, n2),
             V(2, n1, n2), V(2, n1, n2), V(2, 2, 1, n2), V(2, vecs, 1, n2),
             V(2, 2, 1, n2), V(2, 2, 8, n2), V(2, 2, vecs, 1, n2),
+            V(n0, n1, n2), V(2, n1, n2), V(2, n1, n2), V(2, 1, n2), V(2, 1, n2), V(2, vecs, 1, n2), V(vecs, 1, n2),
+            V(8, n2), V(2, 1, n2), V(2, 1, n2), V(2, 8, n2), V(2, 8, n2), V(2, vecs, 1, n2), V(2, vecs, 1, n2),
             *[V(c, 1, n2) for c in counts],
         ]
-        sems = [pltpu.SemaphoreType.DMA(s) for s in ((8,), *[(FIELDS, 3, 2)] * 2, *[(sum(counts),)] * 2, (12,), (12,))]
+        sems = [pltpu.SemaphoreType.DMA(s) for s in ((8,), *[(FIELDS, 3, 2)] * 2, *[(sum(counts),)] * 2, *[(12,)] * 4)]
 
         def scoped(*refs):
             plain, slots_of = refs[: -len(counts)], refs[-len(counts) :]

time: 22.9 us -> 21.2 us (0.926)
  Pallas kernels: 22.8 us -> 21.1 us
    pallas_call x1, Pallas kernels: 21.6 us -> 19.9 us  [local(): pl.pallas_call(scoped, out_shape=[field] * 3 + [pltpu.VMEM(s, f32) for s...]
where the time goes in v5:
time: 21.2 us; the launch traced here: 21.1 us
  Pallas kernels  21.1 us (100%)
    pallas_call x1, Pallas kernels, local(): pl.pallas_call(scoped, out_shape=[field] * 3 + [pltpu.VMEM(s, f32) for s...  19.9 us
    pallas_call x1, Pallas kernels, local(): pl.pallas_call(functools.partial(combine, parts), out_shape=jax.ShapeDtyp...  1.23 us

profile of v5, /device:TPU:0, one launch (start us, length us, event | category | flops | bytes accessed | tf_op | source)
XLA Modules:
  0.0 21.1 jit_solution(4995451849734573410)
XLA Ops:
  0.0 19.9 %shard_map.46 = (f32[3,16,64,128]{3,2,1,0:T(8,128)S(1)}, f32[3,16,64,128]{3,2,1,0:T(8,128)S(1)}, f32[3,16,64,128]{3,2,1,0:T(8,128)S(1)}, f32[8,128]{1,0:T(8,128)...) custom-call(f32[3,16,64,128]{3,2,1,0:T(8,128)} %refs_0_.1, ...), custom_call_target="tpu_custom_call" | custom-call | tf_op jit(solution)/shard_map/pallas_call | solution.py:718
  19.9 1.2 %shard_map.47 = f32[3,16,64,128]{3,2,1,0:T(8,128)} custom-call(f32[3,16,64,128]{3,2,1,0:T(8,128)S(1)} %get-tuple-element.12.OB, f32[3,16,64,128]{3,2,1,0:T(8,128)S(1)} %get-tuple-element.13.G1, f32[3,16,64,128]{3,2,1,0:T(8,128)S(1)} %get-tuple-element.14.G2, f32[8,128]{1,0:T(8,128)S(1)} %get-tuple-element.15.CO, f32[64,128]{1,0:T(8,128)S(1)} %get-tuple-element.16.MZ, ...), custom_call_target="tpu_custom_call" | custom-call | tf_op jit(solution)/shard_map/pallas_call | solution.py:727

commit v6 on v5

--- a/solution.py
+++ b/solution.py
@@ -43,7 +43,7 @@
     res, dia, shf, csh, OB, G1, G2, CO, MZ, MX, MY,
     R, D, NI, CS, S, FG, CI, CR, A1, NL, T, V1, V2, F,
     SX, RX, SY, RY, NZ, CZ, LZX, LXY, RZX, RZY, RXY,
-    P, PZ, NZI, LRZ, LRX, LY2, LY1, LP0, RRZ, RRX, RZ2, RZ0, RX2, RX1,
+    P, PZ, NZI, LRZ, LRX, LY2, LY1, LP0, RRZ, RRX, RZ2, RZ0, RX2, RX1, DX,
     slots_of,
     in_sem, send_sem, recv_sem, psend, precv, lsend, lrecv, csend, crecv,
 ):
@@ -63,26 +63,6 @@
             AXES[a]: lax.rem(me[a] + (o if sign > 0 else sizes[a] - o), sizes[a]) for a, o in zip(axes, offs)
         }
 
-    loads = [pltpu.make_async_copy(shf, NI, in_sem.at[0])]
-    for k in (1, 2, 0):
-        for src, dst in ((res, R), (dia, D)):
-            loads.append(pltpu.make_async_copy(src.at[k], dst.at[k], in_sem.at[len(loads)]))
-    loads.append(pltpu.make_async_copy(csh, CS, in_sem.at[7]))
-    for c in loads:
-        c.start()
-
-    zplane = jnp.zeros((n1, n2), jnp.float32)
-    for k in range(3):
-        S[k, 0, rows] = zplane
-        S[k, n0 + 1, rows] = zplane
-        F[k, n0, 0:n1] = zplane
-        for i in range(n0):
-            F[k, i, n1 : n1 + 1] = jnp.zeros((1, n2), jnp.float32)
-    for V in (V1, V2):
-        V[0, rows] = zplane
-        V[m0 + 1, rows] = zplane
-    for buf in (RX, RY, NZ, CZ, RZX, RZY, RXY, PZ, NZI, RRZ, RRX, RZ2, RZ0, RX2, RX1):
-        buf[...] = jnp.zeros(buf.shape, jnp.float32)
     barrier = pltpu.get_barrier_semaphore()
     faces = [offs for offs in itertools.product((-1, 0, 1), repeat=3) if sum(map(abs, offs)) == 1]
     lines = [offs for offs in itertools.product((-1, 0, 1), repeat=3) if sum(map(abs, offs)) == 2]
@@ -103,6 +83,42 @@
             )
         )
         total = total + there.astype(jnp.int32)
+
+    bands = (0, n1 - 8)
+    loads = {}
+
+    def load(key, src, dst):
+        loads[key] = pltpu.make_async_copy(src, dst, in_sem.at[len(loads)])
+        loads[key].start()
+
+    for first, count in [(r, 8) for r in bands] + [(8, n1 - 16)]:
+        at = pl.ds(first, count)
+        load((3, first), shf.at[:, at], NI.at[:, at])
+        for k in (1, 2, 0):
+            load((k, first, 0), res.at[k, :, at], R.at[k, :, at])
+            load((k, first, 1), dia.at[k, :, at], D.at[k, :, at])
+    load(4, csh, CS)
+
+    for k in range(3):
+        for i in range(n0):
+            F[k, i, n1 : n1 + 1] = jnp.zeros((1, n2), jnp.float32)
+    DX[...] = jnp.zeros(DX.shape, jnp.float32)
+
+    def clear(offs, *refs):
+        @pl.when(jnp.logical_not(exists(offs)))
+        def _():
+            for ref in refs:
+                ref[...] = jnp.zeros(ref.shape, jnp.float32)
+
+    for d in (0, 1):
+        step, i, c = (1, n0 + 1, m0 + 1) if d else (-1, 0, 0)
+        planes = [S.at[k, i, rows] for k in range(3)] + [V1.at[c, rows], NZ.at[d], CZ.at[d], PZ.at[d], NZI.at[d]]
+        clear((step, 0, 0), *planes, *([F.at[k, n0, pl.ds(0, n1)] for k in range(3)] if d else []))
+        clear((0, step, 0), *[RX.at[f, d] for f in range(FIELDS) if f not in LOCAL])
+        clear((0, 0, step), *[RY.at[f, d] for f in range(FIELDS) if f not in LOCAL])
+    for offs in lines:
+        z, x, y = [int(o > 0) for o in offs]
+        clear(offs, RXY.at[x, y] if not offs[0] else RZY.at[z, y] if not offs[1] else RZX.at[z, x])
 
     lane = lax.broadcasted_iota(jnp.int32, (8, n2), 1)
     lane_full = lax.broadcasted_iota(jnp.int32, (n1, n2), 1)
@@ -210,12 +226,12 @@
     def can_send(a, d):
         return me[a] < sizes[a] - 1 if d else me[a] > 0
 
-    def send(f, a):
-        for d in dirs(f):
+    def send(f, a, only=(0, 1)):
+        for d in [d for d in dirs(f) if d in only]:
             pl.when(can_send(a, d))(lambda f=f, a=a, d=d: message(f, a, d).start())
 
-    def receive(f, a):
-        for d in dirs(f):
+    def receive(f, a, only=(0, 1)):
+        for d in [d for d in dirs(f) if d in only]:
             pl.when(can_send(a, 1 - d))(lambda f=f, a=a, d=d: message(f, a, d).wait_recv())
 
     def faces_x(f, get, count):
@@ -267,22 +283,40 @@
         offs[a], offs[b] = (-sign if d else sign), sign
         return tuple(offs)
 
+    CROSS_INTO = {(0, 1): RRZ, (1, 0): RRX, (0, 2): RZ2, (2, 0): RZ0, (1, 2): RX2, (2, 1): RX1}
+    for a, b, d in CROSS:
+        clear(cross_offs(a, b, d, -1), CROSS_INTO[a, b].at[d])
+
     def cross_rows():
         for d in (0, 1):
             i, r = (0 if d else n0 - 1), (0 if d else n1 - 1)
             LRZ[d] = S[1, 1 + i, PAD + n1 - 1 : PAD + n1]
             LRX[d] = S[0, n0, PAD + r : PAD + r + 1]
-            for v in range(LY2.shape[1]):
-                LY2[d, v] = SY[2, v, (0 if d else 7) : (1 if d else 8)]
+        for k, g in ((2, groups - 1), (2, 0), (1, groups - 1)):
+            top = [((i, g), S[k, 1 + i, PAD + 8 * g : PAD + 8 * g + 8]) for i in range(n0)]
+            for v, acc in gather(top, 2).items():
+                line = acc[7:8] if g else acc[0:1]
+                if k == 2:
+                    LY2[0 if g else 1, v] = line
+                else:
+                    LY1[v] = line
+
+    def cross_plane():
         top = [((n0 - 1, g), S[0, n0, PAD + 8 * g : PAD + 8 * g + 8]) for g in range(groups)]
         for acc in gather(top, 2).values():
             LP0[...] = acc
-        last = [((i, groups - 1), S[1, 1 + i, PAD + n1 - 8 : PAD + n1]) for i in range(n0)]
-        for v, acc in gather(last, 2).items():
-            LY1[v] = acc[7:8]
-
-    def cross_send():
-        for at in CROSS:
+
+    def rows_rhs():
+        rowi = lax.broadcasted_iota(jnp.int32, (n0, n2), 0)
+        lanei = lax.broadcasted_iota(jnp.int32, (n0, n2), 1)
+        inner = [S[1, 1 + i, PAD + n1 - 2 : PAD + n1 - 1] for i in range(n0)]
+        for d in (0, 1):
+            x = jnp.where(rowi >= 1, pltpu.roll(SX[0, d], 1, 0), 0.0) - SX[0, d]
+            x = x + jnp.where(lanei >= 1, pltpu.roll(SX[2, d], 1, 1), 0.0) - SX[2, d]
+            SX[PI, d] = x - SX[1, d] + jnp.concatenate(inner, axis=0) if d else x - SX[1, d]
+
+    def cross_send(which):
+        for at in [at for at in CROSS if (at[:2] in ((0, 2), (2, 0))) == which]:
             pl.when(exists(cross_offs(*at, 1)))(lambda at=at: cross_message(*at, 1).start())
 
     def cross_receive():
@@ -324,15 +358,8 @@
             ws.append((rhs + jnp.where(here, line, 0.0)) * en)
         return ws
 
-    def lines_send():
-        for z in (0, 1):
-            for x in (0, 1):
-                c, r = (m0 - 1) * z, (n1 - 1) * x
-                LZX[z, x] = V1[1 + c, PAD + r : PAD + r + 1]
-        for x in (0, 1):
-            for v in range(LXY.shape[1]):
-                LXY[x, v] = SY[V1I, v, 7 * x : 7 * x + 1]
-        for offs in lines:
+    def lines_send(which):
+        for offs in [offs for offs in lines if which(offs)]:
             pl.when(exists(offs))(lambda offs=offs: line_message(offs, 1).start())
 
     def lines_receive():
@@ -392,21 +419,11 @@
             ws.append(ev[v] - eci[v] * near)
         return ws
 
-    def exchange(f, p):
+    def one(f, a, only=(0, 1)):
         ref, count = field(f)
-        send(f, 0)
-        faces_x(f, lambda i, r: ref[1 + i, PAD + r : PAD + r + 1], count)
-        send(f, 1)
-        pack(f, lambda i: ref[1 + i, rows], count, p)
-        send(f, 2)
-
-    def one(f, a):
-        ref, count = field(f)
-        if a == 1:
-            faces_x(f, lambda i, r: ref[1 + i, PAD + r : PAD + r + 1], count)
         if a == 2:
             pack(f, lambda i: ref[1 + i, rows], count, 2)
-        send(f, a)
+        send(f, a, only)
 
     def spread_faces(f, ref, n, p):
         send(f, 0)
@@ -425,51 +442,65 @@
                 rhs = rhs + S[0, i, rows]
             P[i] = rhs
 
-    loads[0].wait()
-    for i in range(n0):
-        NI[i] = 1.0 / (6.0 + NI[i])
-    for pos, (k, a) in enumerate(((1, 1), (2, 2), (0, 0))):
-        loads[1 + 2 * pos].wait()
-        loads[2 + 2 * pos].wait()
-        for i in range(n0):
-            inv = 1.0 / D[k, i]
-            D[k, i] = inv
-            S[k, 1 + i, rows] = R[k, i] * inv
-        if pos == 0:
-            pl.semaphore_wait(barrier, total)
-            spread_faces(NII, NI, n0, 2)
-        one(k, a)
+    def invert(first, count):
+        at = pl.ds(first, count)
+        loads[3, first].wait()
+        NI[:, at] = 1.0 / (6.0 + NI[:, at])
+
+    def scale(k, first, count):
+        at = pl.ds(first, count)
+        for part in (0, 1):
+            loads[k, first, part].wait()
+        inv = 1.0 / D[k, :, at]
+        D[k, :, at] = inv
+        S[k, pl.ds(1, n0), pl.ds(PAD + first, count)] = R[k, :, at] * inv
+
+    for first in bands:
+        invert(first, 8)
+    faces_x(NII, lambda i, r: NI[i, r : r + 1], n0)
+    for k in (1, 2, 0):
+        for first in bands:
+            scale(k, first, 8)
+        faces_x(k, lambda i, r: S[k, 1 + i, PAD + r : PAD + r + 1], n0)
+    cross_rows()
+    rows_rhs()
+    pl.semaphore_wait(barrier, total)
+    cross_send(False)
+    send(1, 1, (1,))
+    send(PI, 1)
+    send(NII, 1)
+    invert(8, n1 - 16)
+    send(NII, 0)
+    pack(NII, lambda i: NI[i], n0, 2)
+    send(NII, 2)
+    for k in (1, 2, 0):
+        scale(k, 8, n1 - 16)
+        if k == 2:
+            pack(2, lambda i: S[2, 1 + i, rows], n0, 2)
+            send(2, 2, (1,))
+    send(0, 0, (1,))
+    cross_plane()
+    cross_send(True)
     partial_rhs()
-    cross_rows()
-    cross_send()
-    spread_faces(PI, P, n0, 2)
-    for f, a in ((0, 1), (2, 1), (1, 0), (2, 0), (0, 2), (1, 2)):
-        one(f, a)
-
-    loads[7].wait()
-    spread_rows = (
-        lax.broadcasted_iota(jnp.int32, (n1, m1), 0) // 2 == lax.broadcasted_iota(jnp.int32, (n1, m1), 1)
-    ).astype(jnp.float32)
+    send(PI, 0)
+    pack(PI, lambda i: P[i], n0, 2)
+    send(PI, 2)
+    loads[4].wait()
     spread_cols = (
         lax.broadcasted_iota(jnp.int32, (m2, n2), 1) // 2 == lax.broadcasted_iota(jnp.int32, (m2, n2), 0)
     ).astype(jnp.float32)
-    exact = functools.partial(
-        jnp.dot, precision=lax.Precision.HIGHEST, preferred_element_type=jnp.float32
-    )
-    for i in range(m0):
-        CI[i] = exact(spread_rows, exact(1.0 / (6.0 + CS[i]), spread_cols))
+    inverse = (1.0 / (6.0 + CS[...])).reshape(m0 * m1, m2)
+    inverse = jnp.dot(
+        inverse, spread_cols, precision=lax.Precision.HIGHEST, preferred_element_type=jnp.float32
+    ).reshape(m0, m1, n2)
+    for c in range(m0):
+        for r in (0, 1):
+            CI[c, pl.ds(r, m1, stride=2)] = inverse[c]
     spread_faces(CII, CI, m0, 4)
 
-    receive(1, 1)
-    receive(0, 0)
-    receive(2, 2)
-    ws = edges(2, 2)
     for i in range(n0):
-        rhs = P[i] + jnp.where(lane_full < 1, halo(ws, i, 2), 0.0)
-        if i == 0:
-            rhs = rhs + S[0, 0, rows]
-        first = rhs[0:8] + jnp.where(row8 < 1, RX[1, 0, i : i + 1], 0.0)
-        FG[1 + i, rows] = jnp.concatenate([first, rhs[8:]], axis=0) * NI[i]
+        FG[1 + i, rows] = P[i] * NI[i]
+
     def gradients(j, G):
         for i in range(n0):
             x = F[j, i, 0:n1]
@@ -481,8 +512,7 @@
 
     def smooth(k):
         for a in range(3):
-            if (k, a) not in ((1, 1), (0, 0), (2, 2)):
-                receive(k, a)
+            receive(k, a, (0,) if (k, a) in from_low else (0, 1))
         rows_x(k, S.at[k])
         w = edges(k, 2)
         for i in range(n0):
@@ -493,27 +523,103 @@
     for i in range(n0):
         F[0, i, 0:n1] = local_near(FG, i, n0, 1)
 
+    def pair_rows(t, slot):
+        t = t + jnp.where(lane_full % 2 == 0, pltpu.roll(t, n2 - 1, 1), pltpu.roll(t, 1, 1))
+        T[slot, rows] = t
+        return t + jnp.where(row_full % 2 == 0, T[slot, pl.ds(PAD + 1, n1)], T[slot, pl.ds(PAD - 1, n1)])
+
+    for c in range(m0):
+        CR[c] = pair_rows(F[0, 2 * c, 0:n1] + F[0, 2 * c + 1, 0:n1], c)
+    from_low = ((0, 0), (1, 1), (2, 2))
+    for f, a in from_low:
+        receive(f, a, (1,))
+    low2 = [jnp.where(is_low[2], 0.0, pltpu.roll(RY[2, 0, v], 1, 1)) for v in range(RY.shape[2])]
+    add = S[0, 0, rows] * NI[0]
+    T[2, rows] = add
+    t = add + jnp.where(row_full >= 1, T[2, pl.ds(PAD - 1, n1)], 0.0)
+    t = t + jnp.where(row_full < n1 - 1, T[2, pl.ds(PAD + 1, n1)], 0.0)
+    t = t + jnp.where(lane_full >= 1, pltpu.roll(add, 1, 1), 0.0)
+    t = t + jnp.where(lane_full < n2 - 1, pltpu.roll(add, n2 - 1, 1), 0.0)
+    A1[0] = t
+    lanei = lax.broadcasted_iota(jnp.int32, (n0, n2), 1)
+    add = RX[1, 0] * SX[NII, 0]
+    DX[pl.ds(PAD, n0)] = add
+    x = add + DX[pl.ds(PAD - 1, n0)] + DX[pl.ds(PAD + 1, n0)]
+    x = x + jnp.where(lanei >= 1, pltpu.roll(add, 1, 1), 0.0)
+    SX[FGI, 0] = x + jnp.where(lanei < n2 - 1, pltpu.roll(add, n2 - 1, 1), 0.0)
+    adds = [e * SY[NII, v] for v, e in enumerate(low2)]
+    group, hop, per = lax.rem(keys[2], groups), 2 * groups, n2 // 2
+    source = 2 * (2 * groups * (keys[4] // groups) + keys[4] % groups) + n2 - is_low[4].astype(jnp.int32)
+    source = lax.rem(source, n2)
+    spread = []
+    for v, add in enumerate(adds):
+        ahead = jnp.where(group < groups - 1, pltpu.roll(pltpu.roll(add, n2 - 2, 1), 7, 0), 0.0)
+        behind = jnp.where(group > 0, pltpu.roll(pltpu.roll(add, 2, 1), 1, 0), 0.0)
+        w = add + jnp.where(row8 < 7, pltpu.roll(add, 7, 0), ahead)
+        w = w + jnp.where(row8 > 0, pltpu.roll(add, 1, 0), behind)
+        ahead = pltpu.roll(adds[v + 1], n2 - hop, 1) if v + 1 < len(adds) else 0.0
+        behind = pltpu.roll(adds[v - 1], hop, 1) if v else 0.0
+        w = w + jnp.where(keys[2] < per - groups, pltpu.roll(add, n2 - hop, 1), ahead)
+        w = w + jnp.where(keys[2] >= groups, pltpu.roll(add, hop, 1), behind)
+        spread.append(w)
     for f in (NII, PI):
         for a in range(3):
             receive(f, a)
     cross_receive()
     ws = halo_fg()
+    CR[0] = CR[0] + pair_rows(FG[0, rows] + A1[0], 0)
+    CR[m0 - 1] = CR[m0 - 1] + pair_rows(FG[n0 + 1, rows], 1)
+    SX[FGI, 0] = SX[FGI, 0] + RX[FGI, 0]
+    SX[FGI, 1] = RX[FGI, 1]
+    even = lax.broadcasted_iota(jnp.int32, (m0, n2), 1) % 2 == 0
+    for d in (0, 1):
+        x = SX[FGI, d, pl.ds(0, m0, stride=2)] + SX[FGI, d, pl.ds(1, m0, stride=2)]
+        RX[V2I, d, 0:m0] = x + jnp.where(even, pltpu.roll(x, n2 - 1, 1), pltpu.roll(x, 1, 1))
+    blocks = []
+    for v, (w, add) in enumerate(zip(ws, spread)):
+        w = w + add
+        w = w + pltpu.roll(w, n2 - hop, 1)
+        w = w + jnp.where(row8 % 2 == 0, pltpu.roll(w, 7, 0), pltpu.roll(w, 1, 0))
+        blocks.append(jnp.take_along_axis(w, source, axis=1))
+    side = (lane_full < 2) | (lane_full >= n2 - 2)
     for c in range(m0):
-        t = None
-        for i in (2 * c, 2 * c + 1):
-            near = outer_near(F[0, i, 0:n1], FG, FGI, ws, i, n0, 2)
-            F[0, i, 0:n1] = near
-            t = near if t is None else t + near
-        t = t + jnp.where(lane_full % 2 == 0, pltpu.roll(t, n2 - 1, 1), pltpu.roll(t, 1, 1))
-        T[c, rows] = t
-        t = t + jnp.where(row_full % 2 == 0, T[c, pl.ds(PAD + 1, n1)], T[c, pl.ds(PAD - 1, n1)])
+        t = CR[c] + jnp.where(side, halo(blocks, c, 4), 0.0)
+        low = t[0:8] + jnp.where(row8 < 2, RX[V2I, 0, c : c + 1], 0.0)
+        high = t[n1 - 8 : n1] + jnp.where(row8 >= 6, RX[V2I, 1, c : c + 1], 0.0)
+        t = jnp.concatenate([low, t[8 : n1 - 8], high], axis=0)
         CR[c] = t
         V1[1 + c, rows] = t * CI[c]
-    exchange(V1I, 4)
-    lines_send()
+    rowc = lax.broadcasted_iota(jnp.int32, (m0, n2), 0)
+    lanec = lax.broadcasted_iota(jnp.int32, (m0, n2), 1)
+    faces_x(V1I, lambda c, r: V1[1 + c, PAD + r : PAD + r + 1], m0)
+    for z in (0, 1):
+        for x in (0, 1):
+            c = (m0 - 1) * z
+            LZX[z, x] = SX[V1I, x, c : c + 1]
+    for x in (0, 1):
+        g = (groups - 1) * x
+        ends = [((c, g), V1[1 + c, PAD + 8 * g : PAD + 8 * g + 8]) for c in range(m0)]
+        for v, acc in gather(ends, 4).items():
+            LXY[x, v] = acc[7 * x : 7 * x + 1]
+    lines_send(lambda offs: offs[1] != 0)
+    send(V1I, 1)
+    for d, r in ((0, 2), (1, n1 - 3)):
+        x = SX[V1I, d, 0:m0]
+        near = jnp.concatenate([V1[1 + c, PAD + r : PAD + r + 1] for c in range(m0)], axis=0)
+        near = near + jnp.where(rowc >= 1, pltpu.roll(x, 1, 0), 0.0)
+        near = near + jnp.where(rowc < m0 - 1, pltpu.roll(x, m0 - 1, 0), 0.0)
+        near = near + jnp.where(lanec >= 2, pltpu.roll(x, 2, 1), 0.0)
+        SX[NLI, d, 0:m0] = near + jnp.where(lanec < n2 - 2, pltpu.roll(x, n2 - 2, 1), 0.0)
+    send(NLI, 1)
+    send(V1I, 0)
+    pack(V1I, lambda c: V1[1 + c, rows], m0, 4)
+    lines_send(lambda offs: offs[1] == 0)
+    send(V1I, 2)
     for c in range(m0):
         NL[c] = local_near(V1, c, m0, 2)
-    spread_faces(NLI, NL, m0, 4)
+    send(NLI, 0)
+    pack(NLI, lambda c: NL[c], m0, 4)
+    send(NLI, 2)
 
     def faces_f(j):
         f = F0I + j
@@ -523,16 +629,35 @@
         pack(f, lambda i: F[j, i, 0:n1], n0, 2)
         send(f, 2)
 
+    for f, a in ((0, 1), (2, 1), (1, 0), (2, 0), (0, 2), (1, 2)):
+        one(f, a)
+    for f, a in from_low:
+        send(f, a, (0,))
     for i in range(n0):
-        F[0, i, 0:n1] = FG[1 + i, rows] + F[0, i, 0:n1] * NI[i]
+        rhs = P[i] + jnp.where(lane_full < 1, halo(low2, i, 2), 0.0)
+        if i == 0:
+            rhs = rhs + S[0, 0, rows]
+        first = rhs[0:8] + jnp.where(row8 < 1, RX[1, 0, i : i + 1], 0.0)
+        FG[1 + i, rows] = jnp.concatenate([first, rhs[8:]], axis=0) * NI[i]
+    for i in range(n0):
+        near = outer_near(local_near(FG, i, n0, 1), FG, FGI, ws, i, n0, 2)
+        F[0, i, 0:n1] = FG[1 + i, rows] + near * NI[i]
     faces_f(0)
-    for k in (1, 2, 0):
-        smooth(k)
-    gradients(0, OB)
+
+    def fold(x):
+        acc = x[0:8]
+        for g in range(1, groups):
+            acc = acc + x[8 * g : 8 * g + 8]
+        return acc
+
+    sums = [jnp.zeros((8, n2), jnp.float32) for _ in range(4)]
+    for c in range(m0):
+        sums[0] = sums[0] + fold(V1[1 + c, rows] * CR[c])
 
     for f in (CII, V1I, NLI):
         for a in range(3):
             receive(f, a)
+    lines_receive()
     ws = edges(V1I, 4)
     for c in range(m0):
         near = outer_near(NL[c], V1, V1I, ws, c, m0, 4)
@@ -540,14 +665,7 @@
         V2[1 + c, rows] = V1[1 + c, rows] - near * CI[c]
     faces_x(V2I, lambda c, r: V2[1 + c, PAD + r : PAD + r + 1], m0)
     pack(V2I, lambda c: V2[1 + c, rows], m0, 4)
-    lines_receive()
     w2 = halo_v2(ws, edges(NLI, 4), edges(CII, 4))
-
-    def fold(x):
-        acc = x[0:8]
-        for g in range(1, groups):
-            acc = acc + x[8 * g : 8 * g + 8]
-        return acc
 
     def spread_near(j, V, w):
         for c in range(m0):
@@ -557,21 +675,22 @@
             F[j, 2 * c + 1, 0:n1] = (near + V[c + 2, rows]) * NI[2 * c + 1]
         faces_f(j)
 
-    sums = [jnp.zeros((8, n2), jnp.float32) for _ in range(5)]
     for c in range(m0):
-        v1, v2, a1, cr = V1[1 + c, rows], V2[1 + c, rows], A1[c], CR[c]
-        sums[0] = sums[0] + fold(v1 * cr)
-        sums[1] = sums[1] + fold(v2 * cr)
-        sums[2] = sums[2] + fold(v1 * a1)
-        sums[3] = sums[3] + fold(v2 * a1)
-        sums[4] = sums[4] + fold(v2 * (a1 - local_near(V2, c, m0, 2)))
+        v1, v2, a1 = V1[1 + c, rows], V2[1 + c, rows], A1[c]
+        near = jnp.where(row_full < n1 - 2, V2[1 + c, pl.ds(PAD + 2, n1)], 0.0)
+        near = near + jnp.where(lane_full < n2 - 2, pltpu.roll(v2, n2 - 2, 1), 0.0)
+        if c < m0 - 1:
+            near = near + V2[2 + c, rows]
+        sums[1] = sums[1] + fold(v1 * a1)
+        sums[2] = sums[2] + fold(v2 * a1)
+        sums[3] = sums[3] + fold(v2 * (a1 - 2.0 * near))
     outer = fold(V2[1, rows] * V2[0, rows] + V2[m0, rows] * V2[m0 + 1, rows])
     for v, w in enumerate(w2):
         outer = outer + SY[V2I, v] * w
     rim = SX[V2I, 0, 0:m0] * RX[V2I, 0, 0:m0] + SX[V2I, 1, 0:m0] * RX[V2I, 1, 0:m0]
-    sums[4] = sums[4] - outer
+    sums[3] = sums[3] - outer
     rim = 2.0 * jnp.sum(rim, axis=0, keepdims=True)
-    sums[4] = sums[4] - jnp.where(row8 == 0, rim, 0.0)
+    sums[3] = sums[3] - jnp.where(row8 == 0, rim, 0.0)
     lane1 = lax.broadcasted_iota(jnp.int32, (1, n2), 1)
     part = jnp.zeros((1, n2), jnp.float32)
     for q, s in enumerate(sums):
@@ -613,15 +732,33 @@
     spread_near(1, V1, ws)
     gradients(1, G1)
     gradients(2, G2)
+    for k in (1, 2, 0):
+        smooth(k)
+    gradients(0, OB)
+
+    def drain(fields):
+        for a in range(3):
+            for d in (0, 1):
+                def over(a=a, d=d):
+                    for f in fields:
+                        if f not in LOCAL and d in dirs(f):
+                            message(f, a, d).wait_send()
+                pl.when(can_send(a, d))(over)
+
+    drain([f for f in range(FIELDS) if f not in FINAL])
+    for offs in lines:
+        pl.when(exists(offs))(lambda offs=offs: line_message(offs, 1).wait_send())
+    for at in CROSS:
+        pl.when(exists(cross_offs(*at, 1)))(lambda at=at: cross_message(*at, 1).wait_send())
 
     part = sum_end(0)
     for p in range(1, len(phases)):
         sum_start(p, part)
         part = sum_end(p)
-    gone, gtwo, hone, hmix, htwo = [
-        jnp.sum(jnp.where(lane1 == q, part, 0.0), axis=1, keepdims=True) for q in range(5)
+    gone, hone, hmix, htwo = [
+        jnp.sum(jnp.where(lane1 == q, part, 0.0), axis=1, keepdims=True) for q in range(4)
     ]
-    two = (gtwo - hmix * gone / hone) / (htwo - hmix * hmix / hone)
+    two = (hone - hmix * gone / hone) / (htwo - hmix * hmix / hone)
     oneco = (gone - hmix * two) / hone
     CO[0:1] = jnp.broadcast_to(oneco, (1, n2))
     CO[1:2] = jnp.broadcast_to(two, (1, n2))
@@ -641,17 +778,7 @@
     for p in range(len(phases)):
         for offs in offsets(phases[p]):
             sum_message(p, offs, 1).wait_send()
-    for offs in lines:
-        pl.when(exists(offs))(lambda offs=offs: line_message(offs, 1).wait_send())
-    for at in CROSS:
-        pl.when(exists(cross_offs(*at, 1)))(lambda at=at: cross_message(*at, 1).wait_send())
-    for a in range(3):
-        for d in (0, 1):
-            def drain(a=a, d=d):
-                for f in range(FIELDS):
-                    if f not in LOCAL and d in dirs(f):
-                        message(f, a, d).wait_send()
-            pl.when(can_send(a, d))(drain)
+    drain(FINAL)
 
 
 def combine(parts, OB, G1, G2, CO, MZ, MX, MY, out, W, sem):
@@ -704,10 +831,10 @@
             V(2, n1, n2), V(2, n1, n2), V(2, 2, 1, n2), V(2, vecs, 1, n2),
             V(2, 2, 1, n2), V(2, 2, 8, n2), V(2, 2, vecs, 1, n2),
             V(n0, n1, n2), V(2, n1, n2), V(2, n1, n2), V(2, 1, n2), V(2, 1, n2), V(2, vecs, 1, n2), V(vecs, 1, n2),
-            V(8, n2), V(2, 1, n2), V(2, 1, n2), V(2, 8, n2), V(2, 8, n2), V(2, vecs, 1, n2), V(2, vecs, 1, n2),
+            V(8, n2), V(2, 1, n2), V(2, 1, n2), V(2, 8, n2), V(2, 8, n2), V(2, vecs, 1, n2), V(2, vecs, 1, n2), V(n0 + 2 * PAD, n2),
             *[V(c, 1, n2) for c in counts],
         ]
-        sems = [pltpu.SemaphoreType.DMA(s) for s in ((8,), *[(FIELDS, 3, 2)] * 2, *[(sum(counts),)] * 2, *[(12,)] * 4)]
+        sems = [pltpu.SemaphoreType.DMA(s) for s in ((22,), *[(FIELDS, 3, 2)] * 2, *[(sum(counts),)] * 2, *[(12,)] * 4)]
 
         def scoped(*refs):
             plain, slots_of = refs[: -len(counts)], refs[-len(counts) :]

time: 21.2 us -> 20.4 us (0.962)
  Pallas kernels: 21.1 us -> 20.3 us
    pallas_call x1, Pallas kernels: 19.9 us -> 19 us  [local(): pl.pallas_call(scoped, out_shape=[field] * 3 + [pltpu.VMEM(s, f32) for s...]
where the time goes in v6:
time: 20.4 us; the launch traced here: 20.3 us
  Pallas kernels  20.3 us (100%)
    pallas_call x1, Pallas kernels, local(): pl.pallas_call(scoped, out_shape=[field] * 3 + [pltpu.VMEM(s, f32) for s...  19 us
    pallas_call x1, Pallas kernels, local(): pl.pallas_call(functools.partial(combine, parts), out_shape=jax.ShapeDtyp...  1.23 us

profile of v6, /device:TPU:0, one launch (start us, length us, event | category | flops | bytes accessed | tf_op | source)
XLA Modules:
  0.0 20.3 jit_solution(12511631728775950184)
XLA Ops:
  0.0 19.0 %shard_map.46 = (f32[3,16,64,128]{3,2,1,0:T(8,128)S(1)}, f32[3,16,64,128]{3,2,1,0:T(8,128)S(1)}, f32[3,16,64,128]{3,2,1,0:T(8,128)S(1)}, f32[8,128]{1,0:T(8,128)...) custom-call(f32[3,16,64,128]{3,2,1,0:T(8,128)} %refs_0_.1, ...), custom_call_target="tpu_custom_call" | custom-call | tf_op jit(solution)/shard_map/pallas_call | solution.py:845
  19.1 1.2 %shard_map.47 = f32[3,16,64,128]{3,2,1,0:T(8,128)} custom-call(f32[3,16,64,128]{3,2,1,0:T(8,128)S(1)} %get-tuple-element.12.OB, f32[3,16,64,128]{3,2,1,0:T(8,128)S(1)} %get-tuple-element.13.G1, f32[3,16,64,128]{3,2,1,0:T(8,128)S(1)} %get-tuple-element.14.G2, f32[8,128]{1,0:T(8,128)S(1)} %get-tuple-element.15.CO, f32[64,128]{1,0:T(8,128)S(1)} %get-tuple-element.16.MZ, ...), custom_call_target="tpu_custom_call" | custom-call | tf_op jit(solution)/shard_map/pallas_call | solution.py:854

commit v7 on v6

--- a/solution.py
+++ b/solution.py
@@ -17,16 +17,21 @@
 COARSE = (V1I, V2I, NLI, CII)
 LOCAL = (V2I, FGI)
 CROSS = [(a, b, d) for a in range(3) for b in range(3) if a != b for d in (0, 1)]
+GREET = [(a, b, 2) for a in range(3) for b in range(a)]
 PAD = 8
 FEW = 32
 
 
+def fence():
+    pl.delay(1)
+
+
 def phases_of(sizes):
     return ((0, 1, 2),) if math.prod(sizes) <= FEW else ((1, 2), (0,))
 
 
 def greeted(sizes, rounds):
-    near = set(itertools.product(range(-1, 2), range(-2, 3), range(-2, 3)))
+    near = set(itertools.product((-1, 0, 1), repeat=3))
     known = set(near)
     for moves in rounds:
         known |= {tuple(p + q for p, q in zip(k, m)) for k in known for m in moves}
@@ -43,7 +48,7 @@
     res, dia, shf, csh, OB, G1, G2, CO, MZ, MX, MY,
     R, D, NI, CS, S, FG, CI, CR, A1, NL, T, V1, V2, F,
     SX, RX, SY, RY, NZ, CZ, LZX, LXY, RZX, RZY, RXY,
-    P, PZ, NZI, LRZ, LRX, LY2, LY1, LP0, RRZ, RRX, RZ2, RZ0, RX2, RX1, DX,
+    P, PZ, NZI, LRZ, LRX, LY2, LY1, LP0, RRZ, RRX, RZ2, RZ0, RX2, RX1, DX, HELLO,
     slots_of,
     in_sem, send_sem, recv_sem, psend, precv, lsend, lrecv, csend, crecv,
 ):
@@ -75,7 +80,7 @@
         return {AXES[a]: me[a] + o for a, o in enumerate(offs) if o}
 
     total = jnp.int32(0)
-    for offs in greeted(sizes, (faces + [m for m in lines if min(m) < 0], faces + lines)):
+    for offs in greeted(sizes, (faces + lines, faces + lines)):
         there = exists(offs)
         pl.when(there)(
             lambda offs=offs: pl.semaphore_signal(
@@ -91,9 +96,9 @@
         loads[key] = pltpu.make_async_copy(src, dst, in_sem.at[len(loads)])
         loads[key].start()
 
+    load(3, shf, NI)
     for first, count in [(r, 8) for r in bands] + [(8, n1 - 16)]:
         at = pl.ds(first, count)
-        load((3, first), shf.at[:, at], NI.at[:, at])
         for k in (1, 2, 0):
             load((k, first, 0), res.at[k, :, at], R.at[k, :, at])
             load((k, first, 1), dia.at[k, :, at], D.at[k, :, at])
@@ -264,7 +269,7 @@
         )
 
     def cross_message(a, b, d, sign):
-        src, dst = {
+        src, dst = (LRZ.at[0], HELLO.at[a + b - 1]) if d == 2 else {
             (0, 1): (LRZ.at[d], RRZ.at[d]),
             (1, 0): (LRX.at[d], RRX.at[d]),
             (0, 2): (SY.at[2, place(0 if d else n0 - 1, 0, 2)[0]], RZ2.at[d]),
@@ -272,7 +277,7 @@
             (1, 2): (LY2.at[d], RX2.at[d]),
             (2, 1): (LY1, RX1.at[d]),
         }[a, b]
-        at = CROSS.index((a, b, d))
+        at = (CROSS + GREET).index((a, b, d))
         return pltpu.make_async_remote_copy(
             src_ref=src, dst_ref=dst, send_sem=csend.at[at], recv_sem=crecv.at[at],
             device_id=device(cross_offs(a, b, d, sign)), device_id_type=MESH,
@@ -280,7 +285,7 @@
 
     def cross_offs(a, b, d, sign):
         offs = [0, 0, 0]
-        offs[a], offs[b] = (-sign if d else sign), sign
+        offs[a], offs[b] = (-sign if d else sign), (-sign if d == 2 else sign)
         return tuple(offs)
 
     CROSS_INTO = {(0, 1): RRZ, (1, 0): RRX, (0, 2): RZ2, (2, 0): RZ0, (1, 2): RX2, (2, 1): RX1}
@@ -316,11 +321,11 @@
             SX[PI, d] = x - SX[1, d] + jnp.concatenate(inner, axis=0) if d else x - SX[1, d]
 
     def cross_send(which):
-        for at in [at for at in CROSS if (at[:2] in ((0, 2), (2, 0))) == which]:
+        for at in [at for at in CROSS + GREET if (at[:2] in ((0, 2), (2, 0)) and at[2] < 2) == which]:
             pl.when(exists(cross_offs(*at, 1)))(lambda at=at: cross_message(*at, 1).start())
 
     def cross_receive():
-        for at in CROSS:
+        for at in CROSS + GREET:
             pl.when(exists(cross_offs(*at, -1)))(lambda at=at: cross_message(*at, -1).wait_recv())
 
     def halo_fg():
@@ -432,20 +437,23 @@
         pack(f, lambda c: ref[c], n, p)
         send(f, 2)
 
-    def partial_rhs():
-        for i in range(n0):
-            x1, x2 = S[1, 1 + i, rows], S[2, 1 + i, rows]
-            rhs = jnp.where(row_full >= 1, S[1, 1 + i, pl.ds(PAD - 1, n1)], 0.0) - x1
-            rhs = rhs + (jnp.where(lane_full >= 1, pltpu.roll(x2, 1, 1), 0.0) - x2)
-            rhs = rhs - S[0, 1 + i, rows]
-            if i > 0:
-                rhs = rhs + S[0, i, rows]
-            P[i] = rhs
-
-    def invert(first, count):
-        at = pl.ds(first, count)
-        loads[3, first].wait()
-        NI[:, at] = 1.0 / (6.0 + NI[:, at])
+    def shifted(i):
+        return jnp.where(lane_full >= 1, pltpu.roll(S[2, 1 + i, rows], 1, 1), 0.0)
+
+    def pack_last():
+        blocks = [((i, g), S[2, 1 + i, PAD + 8 * g : PAD + 8 * g + 8]) for i in range(n0) for g in range(groups)]
+        accs = gather(blocks, 4)
+        half = n2 // 4
+        at = 4 * lax.rem(keys[2], half) + n2
+        found = []
+        for back in (1, 2):
+            source = lax.rem(at - jnp.where(is_low[2], back, 0), n2)
+            for v in range(RY.shape[2]):
+                x, y = [jnp.take_along_axis(accs[min(2 * v + h, len(accs) - 1)], source, axis=1) for h in (0, 1)]
+                found.append(jnp.where(keys[2] < half, x, y))
+        for v in range(RY.shape[2]):
+            SY[2, v] = found[v]
+        return found[RY.shape[2] :]
 
     def scale(k, first, count):
         at = pl.ds(first, count)
@@ -455,9 +463,11 @@
         D[k, :, at] = inv
         S[k, pl.ds(1, n0), pl.ds(PAD + first, count)] = R[k, :, at] * inv
 
-    for first in bands:
-        invert(first, 8)
+    loads[3].wait()
+    for i in range(n0):
+        NI[i] = 1.0 / (6.0 + NI[i])
     faces_x(NII, lambda i, r: NI[i, r : r + 1], n0)
+    pack(NII, lambda i: NI[i], n0, 2)
     for k in (1, 2, 0):
         for first in bands:
             scale(k, first, 8)
@@ -465,26 +475,37 @@
     cross_rows()
     rows_rhs()
     pl.semaphore_wait(barrier, total)
+    fence()
     cross_send(False)
     send(1, 1, (1,))
     send(PI, 1)
     send(NII, 1)
-    invert(8, n1 - 16)
+    send(NII, 2)
     send(NII, 0)
-    pack(NII, lambda i: NI[i], n0, 2)
-    send(NII, 2)
+    fence()
     for k in (1, 2, 0):
         scale(k, 8, n1 - 16)
         if k == 2:
-            pack(2, lambda i: S[2, 1 + i, rows], n0, 2)
+            last2 = pack_last()
             send(2, 2, (1,))
     send(0, 0, (1,))
     cross_plane()
     cross_send(True)
-    partial_rhs()
+    for i in range(n0):
+        x1 = S[1, 1 + i, rows]
+        rhs = jnp.where(row_full >= 1, S[1, 1 + i, pl.ds(PAD - 1, n1)], 0.0) - x1 - S[2, 1 + i, rows]
+        rhs = rhs - S[0, 1 + i, rows]
+        if i > 0:
+            rhs = rhs + S[0, i, rows]
+        P[i] = rhs
+    pack(PI, lambda i: P[i], n0, 2)
+    for v, x in enumerate(last2):
+        SY[PI, v] = SY[PI, v] + jnp.where(is_low[2], x, 0.0)
+    send(PI, 2)
+    for i in (0, n0 - 1):
+        P[i] = P[i] + shifted(i)
     send(PI, 0)
-    pack(PI, lambda i: P[i], n0, 2)
-    send(PI, 2)
+    fence()
     loads[4].wait()
     spread_cols = (
         lax.broadcasted_iota(jnp.int32, (m2, n2), 1) // 2 == lax.broadcasted_iota(jnp.int32, (m2, n2), 0)
@@ -499,6 +520,8 @@
     spread_faces(CII, CI, m0, 4)
 
     for i in range(n0):
+        if 0 < i < n0 - 1:
+            P[i] = P[i] + shifted(i)
         FG[1 + i, rows] = P[i] * NI[i]
 
     def gradients(j, G):
@@ -592,6 +615,7 @@
     rowc = lax.broadcasted_iota(jnp.int32, (m0, n2), 0)
     lanec = lax.broadcasted_iota(jnp.int32, (m0, n2), 1)
     faces_x(V1I, lambda c, r: V1[1 + c, PAD + r : PAD + r + 1], m0)
+    send(V1I, 1)
     for z in (0, 1):
         for x in (0, 1):
             c = (m0 - 1) * z
@@ -602,7 +626,6 @@
         for v, acc in gather(ends, 4).items():
             LXY[x, v] = acc[7 * x : 7 * x + 1]
     lines_send(lambda offs: offs[1] != 0)
-    send(V1I, 1)
     for d, r in ((0, 2), (1, n1 - 3)):
         x = SX[V1I, d, 0:m0]
         near = jnp.concatenate([V1[1 + c, PAD + r : PAD + r + 1] for c in range(m0)], axis=0)
@@ -615,11 +638,13 @@
     pack(V1I, lambda c: V1[1 + c, rows], m0, 4)
     lines_send(lambda offs: offs[1] == 0)
     send(V1I, 2)
+    fence()
     for c in range(m0):
         NL[c] = local_near(V1, c, m0, 2)
     send(NLI, 0)
     pack(NLI, lambda c: NL[c], m0, 4)
     send(NLI, 2)
+    fence()
 
     def faces_f(j):
         f = F0I + j
@@ -726,6 +751,7 @@
         return terms[0]
 
     sum_start(0, part)
+    fence()
     rows_x(V2I, V2)
     spread_near(2, V2, w2)
     rows_x(V1I, V1)
@@ -748,7 +774,7 @@
     drain([f for f in range(FIELDS) if f not in FINAL])
     for offs in lines:
         pl.when(exists(offs))(lambda offs=offs: line_message(offs, 1).wait_send())
-    for at in CROSS:
+    for at in CROSS + GREET:
         pl.when(exists(cross_offs(*at, 1)))(lambda at=at: cross_message(*at, 1).wait_send())
 
     part = sum_end(0)
@@ -831,10 +857,10 @@
             V(2, n1, n2), V(2, n1, n2), V(2, 2, 1, n2), V(2, vecs, 1, n2),
             V(2, 2, 1, n2), V(2, 2, 8, n2), V(2, 2, vecs, 1, n2),
             V(n0, n1, n2), V(2, n1, n2), V(2, n1, n2), V(2, 1, n2), V(2, 1, n2), V(2, vecs, 1, n2), V(vecs, 1, n2),
-            V(8, n2), V(2, 1, n2), V(2, 1, n2), V(2, 8, n2), V(2, 8, n2), V(2, vecs, 1, n2), V(2, vecs, 1, n2), V(n0 + 2 * PAD, n2),
+            V(8, n2), V(2, 1, n2), V(2, 1, n2), V(2, 8, n2), V(2, 8, n2), V(2, vecs, 1, n2), V(2, vecs, 1, n2), V(n0 + 2 * PAD, n2), V(3, 1, n2),
             *[V(c, 1, n2) for c in counts],
         ]
-        sems = [pltpu.SemaphoreType.DMA(s) for s in ((22,), *[(FIELDS, 3, 2)] * 2, *[(sum(counts),)] * 2, *[(12,)] * 4)]
+        sems = [pltpu.SemaphoreType.DMA(s) for s in ((20,), *[(FIELDS, 3, 2)] * 2, *[(sum(counts),)] * 2, *[(12,)] * 2, *[(15,)] * 2)]
 
         def scoped(*refs):
             plain, slots_of = refs[: -len(counts)], refs[-len(counts) :]

time: 20.4 us -> 19.6 us (0.961)
  Pallas kernels: 20.3 us -> 19.4 us
    pallas_call x1, Pallas kernels: 19 us -> 18.2 us  [local(): pl.pallas_call(scoped, out_shape=[field] * 3 + [pltpu.VMEM(s, f32) for s...]
where the time goes in v7:
time: 19.6 us; the launch traced here: 19.4 us
  Pallas kernels  19.4 us (99%)
    pallas_call x1, Pallas kernels, local(): pl.pallas_call(scoped, out_shape=[field] * 3 + [pltpu.VMEM(s, f32) for s...  18.2 us
    pallas_call x1, Pallas kernels, local(): pl.pallas_call(functools.partial(combine, parts), out_shape=jax.ShapeDtyp...  1.23 us

profile of v7, /device:TPU:0, one launch (start us, length us, event | category | flops | bytes accessed | tf_op | source)
XLA Modules:
  0.0 19.4 jit_solution(5706647580095300890)
XLA Ops:
  0.0 18.2 %shard_map.46 = (f32[3,16,64,128]{3,2,1,0:T(8,128)S(1)}, f32[3,16,64,128]{3,2,1,0:T(8,128)S(1)}, f32[3,16,64,128]{3,2,1,0:T(8,128)S(1)}, f32[8,128]{1,0:T(8,128)...) custom-call(f32[3,16,64,128]{3,2,1,0:T(8,128)} %refs_0_.1, ...), custom_call_target="tpu_custom_call" | custom-call | tf_op jit(solution)/shard_map/pallas_call | solution.py:871
  18.2 1.2 %shard_map.47 = f32[3,16,64,128]{3,2,1,0:T(8,128)} custom-call(f32[3,16,64,128]{3,2,1,0:T(8,128)S(1)} %get-tuple-element.12.OB, f32[3,16,64,128]{3,2,1,0:T(8,128)S(1)} %get-tuple-element.13.G1, f32[3,16,64,128]{3,2,1,0:T(8,128)S(1)} %get-tuple-element.14.G2, f32[8,128]{1,0:T(8,128)S(1)} %get-tuple-element.15.CO, f32[64,128]{1,0:T(8,128)S(1)} %get-tuple-element.16.MZ, ...), custom_call_target="tpu_custom_call" | custom-call | tf_op jit(solution)/shard_map/pallas_call | solution.py:880

commit v8 on v7

--- a/solution.py
+++ b/solution.py
@@ -45,7 +45,7 @@
 
 def kernel(
     sizes,
-    res, dia, shf, csh, OB, G1, G2, CO, MZ, MX, MY,
+    res, dia, shf, csh, OB, G1, G2, CO, HZ, HX, HY,
     R, D, NI, CS, S, FG, CI, CR, A1, NL, T, V1, V2, F,
     SX, RX, SY, RY, NZ, CZ, LZX, LXY, RZX, RZY, RXY,
     P, PZ, NZI, LRZ, LRX, LY2, LY1, LP0, RRZ, RRX, RZ2, RZ0, RX2, RX1, DX, HELLO,
@@ -771,16 +771,27 @@
                             message(f, a, d).wait_send()
                 pl.when(can_send(a, d))(over)
 
-    drain([f for f in range(FIELDS) if f not in FINAL])
+    drain(range(FIELDS))
     for offs in lines:
         pl.when(exists(offs))(lambda offs=offs: line_message(offs, 1).wait_send())
     for at in CROSS + GREET:
         pl.when(exists(cross_offs(*at, 1)))(lambda at=at: cross_message(*at, 1).wait_send())
 
+    for offs in offsets(phases[0]):
+        sum_message(0, offs, 1).wait_send()
+    for j, f in enumerate(FINAL):
+        for a in range(3):
+            receive(f, a)
+        HZ[j] = F[j, n0, 0:n1]
+        HX[j] = RX[f, 1]
+        HY[j] = RY[f, 1]
+
     part = sum_end(0)
     for p in range(1, len(phases)):
         sum_start(p, part)
         part = sum_end(p)
+        for offs in offsets(phases[p]):
+            sum_message(p, offs, 1).wait_send()
     gone, hone, hmix, htwo = [
         jnp.sum(jnp.where(lane1 == q, part, 0.0), axis=1, keepdims=True) for q in range(4)
     ]
@@ -788,26 +799,9 @@
     oneco = (gone - hmix * two) / hone
     CO[0:1] = jnp.broadcast_to(oneco, (1, n2))
     CO[1:2] = jnp.broadcast_to(two, (1, n2))
-    for f in FINAL:
-        for a in range(3):
-            receive(f, a)
-
-    def mix(get):
-        a = get(0)
-        return a + jnp.broadcast_to(oneco, a.shape) * get(1) + jnp.broadcast_to(two, a.shape) * get(2)
-
-    MZ[...] = mix(lambda j: F[j, n0, 0:n1])
-    MX[...] = mix(lambda j: RX[F0I + j, 1])
-    for v in range(RY.shape[2]):
-        MY[v] = pltpu.roll(mix(lambda j: RY[F0I + j, 1, v]), n2 - 1, 1)
-
-    for p in range(len(phases)):
-        for offs in offsets(phases[p]):
-            sum_message(p, offs, 1).wait_send()
-    drain(FINAL)
-
-
-def combine(parts, OB, G1, G2, CO, MZ, MX, MY, out, W, sem):
+
+
+def combine(parts, OB, G1, G2, CO, HZ, HX, HY, out, W, sem):
     _, n0, n1, n2 = OB.shape
     one = jnp.broadcast_to(CO[0:1], (n1, n2))
     two = jnp.broadcast_to(CO[1:2], (n1, n2))
@@ -815,14 +809,21 @@
     row8 = lax.broadcasted_iota(jnp.int32, (8, n2), 0)
     lane_full = lax.broadcasted_iota(jnp.int32, (n1, n2), 1)
 
+    def mix(get):
+        a = get(0)
+        c1, c2 = [jnp.broadcast_to(CO[q : q + 1], a.shape) for q in (0, 1)]
+        return a + c1 * get(1) + c2 * get(2)
+
+    ends = [pltpu.roll(mix(lambda j: HY[j, v]), n2 - 1, 1) for v in range(HY.shape[1])]
+
     def edge(k, i, x):
         if k == 0:
-            return x + MZ[...] if i == n0 - 1 else x
+            return x + mix(lambda j: HZ[j]) if i == n0 - 1 else x
         if k == 1:
-            last = x[n1 - 8 : n1] + jnp.where(row8 == 7, MX[i : i + 1], 0.0)
+            last = x[n1 - 8 : n1] + jnp.where(row8 == 7, mix(lambda j: HX[j, i : i + 1]), 0.0)
             return jnp.concatenate([x[0 : n1 - 8], last], axis=0)
         ats = [divmod(i * groups + g, per) for g in range(groups)]
-        parts = [pltpu.roll(MY[v], (n2 - 2 * kk) % n2, 1) for v, kk in ats]
+        parts = [pltpu.roll(ends[v], (n2 - 2 * kk) % n2, 1) for v, kk in ats]
         return x + jnp.where(lane_full >= n2 - 1, jnp.concatenate(parts, axis=0), 0.0)
 
     copies = []
@@ -870,7 +871,7 @@
         limit = 67_043_328 - 12 * math.prod(residual.shape) - 2**18
         fields = pl.pallas_call(
             scoped,
-            out_shape=[field] * 3 + [pltpu.VMEM(s, f32) for s in ((8, n2), (n1, n2), (n0, n2), (vecs, 8, n2))],
+            out_shape=[field] * 3 + [pltpu.VMEM(s, f32) for s in ((8, n2), (3, n1, n2), (3, n0, n2), (3, vecs, 8, n2))],
             in_specs=[pl.BlockSpec(memory_space=pltpu.HBM)] * 4,
             out_specs=[pl.BlockSpec(memory_space=pltpu.VMEM)] * 7,
             scratch_shapes=scratch,

time: 19.6 us -> 19.4 us (0.990)
  no operation moved by 1% of the time
where the time goes in v8:
time: 19.4 us; the launch traced here: 19.3 us
  Pallas kernels  19.3 us (99%)
    pallas_call x1, Pallas kernels, local(): pl.pallas_call(scoped, out_shape=[field] * 3 + [pltpu.VMEM(s, f32) for s...  18 us
    pallas_call x1, Pallas kernels, local(): pl.pallas_call(functools.partial(combine, parts), out_shape=jax.ShapeDtyp...  1.24 us

profile of v8, /device:TPU:0, one launch (start us, length us, event | category | flops | bytes accessed | tf_op | source)
XLA Modules:
  0.0 19.3 jit_solution(10777162845460470615)
XLA Ops:
  0.0 18.0 %shard_map.46 = (f32[3,16,64,128]{3,2,1,0:T(8,128)S(1)}, f32[3,16,64,128]{3,2,1,0:T(8,128)S(1)}, f32[3,16,64,128]{3,2,1,0:T(8,128)S(1)}, f32[8,128]{1,0:T(8,128)...) custom-call(f32[3,16,64,128]{3,2,1,0:T(8,128)} %refs_0_.1, ...), custom_call_target="tpu_custom_call" | custom-call | tf_op jit(solution)/shard_map/pallas_call | solution.py:872
  18.0 1.2 %shard_map.47 = f32[3,16,64,128]{3,2,1,0:T(8,128)} custom-call(f32[3,16,64,128]{3,2,1,0:T(8,128)S(1)} %get-tuple-element.12.OB, f32[3,16,64,128]{3,2,1,0:T(8,128)S(1)} %get-tuple-element.13.G1, f32[3,16,64,128]{3,2,1,0:T(8,128)S(1)} %get-tuple-element.14.G2, f32[8,128]{1,0:T(8,128)S(1)} %get-tuple-element.15.CO, f32[3,64,128]{2,1,0:T(8,128)S(1)} %get-tuple-element.16.HZ, ...), custom_call_target="tpu_custom_call" | custom-call | tf_op jit(solution)/shard_map/pallas_call | solution.py:881

commit v9 on v8

--- a/solution.py
+++ b/solution.py
@@ -616,6 +616,7 @@
     lanec = lax.broadcasted_iota(jnp.int32, (m0, n2), 1)
     faces_x(V1I, lambda c, r: V1[1 + c, PAD + r : PAD + r + 1], m0)
     send(V1I, 1)
+    fence()
     for z in (0, 1):
         for x in (0, 1):
             c = (m0 - 1) * z

time: 19.4 us -> 19.4 us (level)
  no operation moved by 1% of the time
where the time goes in v9:
time: 19.4 us; the launch traced here: 19.2 us
  Pallas kernels  19.2 us (99%)
    pallas_call x1, Pallas kernels, local(): pl.pallas_call(scoped, out_shape=[field] * 3 + [pltpu.VMEM(s, f32) for s...  18 us
    pallas_call x1, Pallas kernels, local(): pl.pallas_call(functools.partial(combine, parts), out_shape=jax.ShapeDtyp...  1.24 us

profile of v9, /device:TPU:0, one launch (start us, length us, event | category | flops | bytes accessed | tf_op | source)
XLA Modules:
  0.0 19.2 jit_solution(5090064670924184753)
XLA Ops:
  0.0 18.0 %shard_map.46 = (f32[3,16,64,128]{3,2,1,0:T(8,128)S(1)}, f32[3,16,64,128]{3,2,1,0:T(8,128)S(1)}, f32[3,16,64,128]{3,2,1,0:T(8,128)S(1)}, f32[8,128]{1,0:T(8,128)...) custom-call(f32[3,16,64,128]{3,2,1,0:T(8,128)} %refs_0_.1, ...), custom_call_target="tpu_custom_call" | custom-call | tf_op jit(solution)/shard_map/pallas_call | solution.py:873
  18.0 1.2 %shard_map.47 = f32[3,16,64,128]{3,2,1,0:T(8,128)} custom-call(f32[3,16,64,128]{3,2,1,0:T(8,128)S(1)} %get-tuple-element.12.OB, f32[3,16,64,128]{3,2,1,0:T(8,128)S(1)} %get-tuple-element.13.G1, f32[3,16,64,128]{3,2,1,0:T(8,128)S(1)} %get-tuple-element.14.G2, f32[8,128]{1,0:T(8,128)S(1)} %get-tuple-element.15.CO, f32[3,64,128]{2,1,0:T(8,128)S(1)} %get-tuple-element.16.HZ, ...), custom_call_target="tpu_custom_call" | custom-call | tf_op jit(solution)/shard_map/pallas_call | solution.py:882
